TPU v7x, 64 devices: a 2x2x8 block of a 4x4x8 slice. The times are simulated.
64 devices in a mesh: data: 4 (over x, y), expert: 16 (over z, core).
Axes of the slice: x: 2, y: 2, z: 8, core: 2. Of those that a mesh axis runs over, the one named last changes fastest.
The devices are a block of a 4x4x8 slice.
Arguments:
- tokens: bfloat16 [8192, 1024], P(('data', 'expert')), parts along dimension 0
- expert_ids: int32 [8192, 8], P(('data', 'expert')), parts along dimension 0
- gate_wts: float32 [8192, 8], P(('data', 'expert')), parts along dimension 0
- dev_slot: int32 [8192, 8], P(('data', 'expert')), parts along dimension 0
- exp_slot: int32 [8192, 8], P(('data', 'expert')), parts along dimension 0
- w_gate: bfloat16 [32, 1024, 512], P('expert')
- w_up: bfloat16 [32, 1024, 512], P('expert')
- w_down: bfloat16 [32, 512, 1024], P('expert')
Outputs:
- output: bfloat16 [8192, 1024], P(('data', 'expert')), parts along dimension 0
There are 4 independent parts. A program takes and returns all parts, laid end to end along the dimension named above; an argument that names none is the same for every part.
All inputs are finite; a program needn't handle non-finite values.
Results may differ from a plain program's by a relative error of at most 0.00784104.
Values are sent between devices in bfloat16 or wider.
A program may use at most 768 MiB of HBM per device.

v0:
```python
import jax
import jax.numpy as jnp
from jax import lax
from jax.sharding import PartitionSpec as P, NamedSharding


def value_a10(tok_dev, top_k, groups, n_experts):
    dev_cap = min(tok_dev, 8 * ((3 * tok_dev * top_k + 16 * groups - 1) // (16 * groups)))
    exp_cap = 8 * ((tok_dev * groups * top_k + 4 * n_experts - 1) // (4 * n_experts))
    return dev_cap, exp_cap


def solution(mesh):
    groups = mesh.shape["expert"]
    row_spec = P(("data", "expert"), None)
    weight_spec = P("expert", None, None)

    def device_layer(tokens, expert_ids, gate_wts, dev_slot, exp_slot, w_gate, w_up, w_down):
        tok_dev, top_k = expert_ids.shape
        d_model = tokens.shape[1]
        e_local = w_gate.shape[0]
        dev_cap, exp_cap = value_a10(tok_dev, top_k, groups, e_local * groups)
        n_rows = groups * dev_cap
        kept_choice = (dev_slot >= 0) & (exp_slot >= 0)
        dest_row = jnp.where(kept_choice, (expert_ids // e_local) * dev_cap + dev_slot, -1)
        row_hit = jnp.arange(n_rows)[:, None, None] == dest_row[None, :, :]
        pick_mat = jnp.any(row_hit, axis=2).astype(jnp.bfloat16)
        send_x = jnp.dot(pick_mat, tokens, preferred_element_type=jnp.float32).astype(jnp.bfloat16)
        ex_hit = (expert_ids % e_local)[:, :, None] == jnp.arange(e_local)
        meta_vals = jnp.stack([gate_wts, (exp_slot + 1).astype(jnp.float32)], axis=-1)
        meta_in = jnp.where(ex_hit[:, :, :, None], meta_vals[:, :, None, :], 0.0)
        send_meta = jnp.einsum("rtk,tkec->rec", row_hit.astype(jnp.float32), meta_in, precision=lax.Precision.HIGHEST)
        recv_x = lax.all_to_all(send_x.reshape(groups, dev_cap, d_model), "expert", 0, 0, tiled=True)
        recv_meta = lax.all_to_all(send_meta.reshape(groups, dev_cap, e_local, 2), "expert", 0, 0, tiled=True)
        recv_x = recv_x.reshape(n_rows, d_model)
        recv_meta = recv_meta.reshape(n_rows, e_local, 2)
        slot_ids = jnp.arange(1, exp_cap + 1).astype(jnp.float32)
        gather_mat = (recv_meta[:, :, 1].T[:, None, :] == slot_ids[:, None]).astype(jnp.bfloat16)
        exp_in = jnp.einsum("esr,rd->esd", gather_mat, recv_x, preferred_element_type=jnp.float32).astype(jnp.bfloat16)
        hid_gate = jnp.einsum("esd,edf->esf", exp_in, w_gate, preferred_element_type=jnp.float32)
        hid_up = jnp.einsum("esd,edf->esf", exp_in, w_up, preferred_element_type=jnp.float32)
        hidden = (jax.nn.silu(hid_gate) * hid_up).astype(jnp.bfloat16)
        exp_out = jnp.einsum("esf,efd->esd", hidden, w_down, preferred_element_type=jnp.float32).astype(jnp.bfloat16)
        scatter_mat = gather_mat * recv_meta[:, :, 0].T.astype(jnp.bfloat16)[:, None, :]
        z_rows = jnp.einsum("esr,esd->rd", scatter_mat, exp_out, preferred_element_type=jnp.float32).astype(jnp.bfloat16)
        back_rows = lax.all_to_all(z_rows.reshape(groups, dev_cap, d_model), "expert", 0, 0, tiled=True)
        moe_out = jnp.einsum("rt,rd->td", pick_mat, back_rows.reshape(n_rows, d_model), preferred_element_type=jnp.float32)
        return moe_out.astype(jnp.bfloat16)

    def moe_layer(tokens, expert_ids, gate_wts, dev_slot, exp_slot, w_gate, w_up, w_down):
        mapped = jax.shard_map(device_layer, mesh=mesh, in_specs=(row_spec,) * 5 + (weight_spec,) * 3, out_specs=row_spec, check_vma=False)
        return mapped(tokens, expert_ids, gate_wts, dev_slot, exp_slot, w_gate, w_up, w_down)

    return moe_layer
```

profile of v0, /device:TPU:21, one launch (start us, length us, event | category | flops | bytes accessed | tf_op | source)
XLA Modules:
  0.0 204.8 jit_solution(15166647456491584345)
XLA Ops:
  0.0 0.0 copy-start
  0.0 0.9 convert_bitcast_fusion
  0.9 0.7 pad_maximum_fusion
  1.6 2.9 %fusion.22 = f32[1536,2,2]{0,2,1:T(2,128)S(1)} fusion(s32[128,8]{0,1:T(8,128)S(1)} %get-tuple-element.6, pred[128,8,2]{0,1,2:T(8,128)(4,1)S(1)} %iota_compare_fusion.1, f32[128,8,2]{0,2,1:T(2,128)S(1)} %copy.20), kind=kOutput, calls=%fused_computation.21 | convolution fusion | flops 77074432 | bytes 38912 | tf_op jit(solution)/shard_map/rtk,tkec->rec/dot_general | solution.py:32
  4.5 0.1 reshape.32
  4.5 0.6 copy.21
  5.2 10.7 %all-to-all-start = ((f32[16,96,2,2]{1,3,2,0:T(2,128)}), f32[16,96,2,2]{1,3,2,0:T(2,128)S(1)}, u32[]{:S(2)}, u32[]{:S(2)}) async-start(f32[16,96,2,2]{1,3,2,0:T(2,128)} %copy.21), calls=%async_computation | async-start | bytes 65536 | tf_op jit(solution)/shard_map/all_to_all | solution.py:34
  15.9 1.0 fusion.8
  16.9 3.6 %convolution_convert_fusion = bf16[1536,1024]{1,0:T(8,128)(2,1)} fusion(pred[1536,128]{1,0:T(8,128)(4,1)S(1)} %fusion.8, bf16[128,1024]{1,0:T(8,128)(2,1)} %param.8), kind=kOutput, calls=%fused_computation.15 | convolution fusion | flops 404226048 | bytes 3604480 | tf_op jit(solution)/shard_map/dot_general | solution.py:28
  20.5 2.5 %all-to-all-done = f32[16,96,2,2]{1,3,2,0:T(2,128)S(1)} async-done(((f32[16,96,2,2]{1,3,2,0:T(2,128)}), f32[16,96,2,2]{1,3,2,0:T(2,128)S(1)}, u32[]{:S(2)}, u32[]{:S(2)}) %all-to-all-start) | async-done | bytes 24608 | tf_op jit(solution)/shard_map/all_to_all | solution.py:34
  23.1 4.8 %all-to-all-start.1 = ((bf16[16,96,1024]{2,1,0:T(8,128)(2,1)}), bf16[16,96,1024]{2,1,0:T(8,128)(2,1)}, u32[]{:S(2)}, u32[]{:S(2)}) async-start(bf16[16,96,1024]{2,1,0:T(8,128)(2,1)} %bitcast.57), calls=%async_computation.1 | async-start | bytes 6291456 | tf_op jit(solution)/shard_map/all_to_all | solution.py:33
  27.9 0.1 reshape.33
  28.0 70.9 %all-to-all-done.1 = bf16[16,96,1024]{2,1,0:T(8,128)(2,1)} async-done(((bf16[16,96,1024]{2,1,0:T(8,128)(2,1)}), bf16[16,96,1024]{2,1,0:T(8,128)(2,1)}, u32[]{:S(2)}, u32[]{:S(2)}) %all-to-all-start.1) | async-done | bytes 3145760 | tf_op jit(solution)/shard_map/all_to_all | solution.py:33
  98.9 0.0 copy-start.1
  98.9 10.0 %fusion.19 = bf16[2,1024,1024]{2,1,0:T(8,128)(2,1)S(1)} fusion(bf16[1536,1024,1]{1,0,2:T(8,128)(2,1)} %bitcast.9, f32[1024]{0:T(1024)S(1)} %add_convert_fusion, f32[2,1536]{1,0:T(2,128)S(1)} %bitcast.60), kind=kOutput, calls=%fused_computation.20 | convolution fusion | flops 6447693824 | bytes 7356416 | tf_op jit(solution)/shard_map/esr,rd->esd/dot_general | solution.py:39
  108.9 0.0 copy-done.1
  108.9 0.0 copy-start.2
  108.9 2.3 %fusion.36 = f32[2,1024,512]{2,1,0:T(8,128)S(1)} fusion(bf16[2,1024,1024]{2,1,0:T(8,128)(2,1)S(1)} %fusion.19, bf16[2,1024,512]{2,1,0:T(8,128)(2,1)S(1)} %copy-done.1), kind=kOutput, calls=%fused_computation.47 | convolution fusion | flops 2147483648 | bytes 10485760 | tf_op jit(solution)/shard_map/esd,edf->esf/dot_general | solution.py:40
  111.3 0.0 copy-done.2
  111.3 2.8 %multiply_convert_fusion = bf16[2,1024,512]{2,1,0:T(8,128)(2,1)S(1)} fusion(f32[2,1024,512]{2,1,0:T(8,128)S(1)} %fusion.36, bf16[2,1024,1024]{2,1,0:T(8,128)(2,1)S(1)} %fusion.19, bf16[2,1024,512]{2,1,0:T(8,128)(2,1)S(1)} %copy-done.2), kind=kOutput, calls=%fused_computation.14 | convolution fusion | flops 2153775104 | bytes 12582912 | tf_op jit(solution)/shard_map/esd,edf->esf/dot_general | solution.py:41
  114.1 0.0 copy-done
  114.1 2.3 %fusion.59 = bf16[2,1024,1024]{2,1,0:T(8,128)(2,1)S(1)} fusion(bf16[2,1024,512]{2,1,0:T(8,128)(2,1)S(1)} %multiply_convert_fusion, bf16[2,512,1024]{2,1,0:T(8,128)(2,1)S(1)} %copy-done), kind=kOutput, calls=%fused_computation.13.clone.clone.clone.2 | convolution fusion | flops 2149580800 | bytes 8388608 | tf_op jit(solution)/shard_map/esf,efd->esd/dot_general | solution.py:43
  116.5 7.2 %bitcast_convert_fusion = bf16[1536,1024]{1,0:T(8,128)(2,1)S(1)} fusion(f32[1024]{0:T(1024)S(1)} %add_convert_fusion, f32[2,1536]{1,0:T(2,128)S(1)} %bitcast.61, bf16[2,1536]{1,0:T(2,128)(2,1)S(1)} %bitcast.62, bf16[2,1024,1024]{2,1,0:T(8,128)(2,1)S(1)} %fusion.59), kind=kOutput, calls=%fused_computation.4 | convolution fusion | flops 6450315264 | bytes 7362560 | tf_op jit(solution)/shard_map/esr,esd->rd/dot_general | solution.py:45
  123.7 79.8 %all_to_all.15 = bf16[16,96,1024]{2,1,0:T(8,128)(2,1)S(1)} all-to-all(bf16[16,96,1024]{2,1,0:T(8,128)(2,1)S(1)} %bitcast.59), channel_id=1, replica_groups=mesh['data'=4,'expert'=16] {'expert'}, dimensions={0} | all-to-all | bytes 6291456 | tf_op jit(solution)/shard_map/all_to_all | solution.py:46
  203.5 1.4 convolution_convert_fusion.1
  (8 shorter events, 0.1 us)
Async XLA Ops:
  0.0 114.1 %copy-start = (bf16[2,512,1024]{2,1,0:T(8,128)(2,1)S(1)}, bf16[2,512,1024]{2,1,0:T(8,128)(2,1)}, u32[]{:S(2)}) copy-start(bf16[2,512,1024]{2,1,0:T(8,128)(2,1)} %param.15) | copy-start | bytes 6291460
  5.2 17.9 %all-to-all-start = ((f32[16,96,2,2]{1,3,2,0:T(2,128)}), f32[16,96,2,2]{1,3,2,0:T(2,128)S(1)}, u32[]{:S(2)}, u32[]{:S(2)}) async-start(f32[16,96,2,2]{1,3,2,0:T(2,128)} %copy.21), calls=%async_computation | async-start | bytes 65536 | tf_op jit(solution)/shard_map/all_to_all | solution.py:34
  23.1 75.8 %all-to-all-start.1 = ((bf16[16,96,1024]{2,1,0:T(8,128)(2,1)}), bf16[16,96,1024]{2,1,0:T(8,128)(2,1)}, u32[]{:S(2)}, u32[]{:S(2)}) async-start(bf16[16,96,1024]{2,1,0:T(8,128)(2,1)} %bitcast.57), calls=%async_computation.1 | async-start | bytes 6291456 | tf_op jit(solution)/shard_map/all_to_all | solution.py:33
  98.9 10.0 %copy-start.1 = (bf16[2,1024,512]{2,1,0:T(8,128)(2,1)S(1)}, bf16[2,1024,512]{2,1,0:T(8,128)(2,1)}, u32[]{:S(2)}) copy-start(bf16[2,1024,512]{2,1,0:T(8,128)(2,1)} %param.13) | copy-start | bytes 6291460
  108.9 2.4 %copy-start.2 = (bf16[2,1024,512]{2,1,0:T(8,128)(2,1)S(1)}, bf16[2,1024,512]{2,1,0:T(8,128)(2,1)}, u32[]{:S(2)}) copy-start(bf16[2,1024,512]{2,1,0:T(8,128)(2,1)} %param.14) | copy-start | bytes 6291460
where the time goes:
time: 205 us
  blocking collectives  79.8 us (39%)
  waiting for transfers between devices  73.4 us (36%)
  matrix products  32.5 us (16%)
  starting transfers between devices  15.5 us (8%)
  other arithmetic  2.6 us (1%)
    all_to_all x1, blocking collectives, device_layer(): lax.all_to_all(z_rows.reshape(groups, dev_cap, d_model), 'expert', 0, 0,...  79.8 us
    all_to_all x1, waiting for transfers between devices, device_layer(): lax.all_to_all(send_x.reshape(groups, dev_cap, d_model), 'expert', 0, 0,...  70.9 us
    all_to_all x1, starting transfers between devices, device_layer(): lax.all_to_all(send_meta.reshape(groups, dev_cap, e_local, 2), 'expert',...  10.7 us
    dot_general x1, matrix products, device_layer(): jnp.einsum('esr,rd->esd', gather_mat, recv_x, preferred_element_type=jnp....  10 us
    dot_general x1, matrix products, device_layer(): jnp.einsum('esr,esd->rd', scatter_mat, exp_out, preferred_element_type=jn...  7.24 us
    all_to_all x1, starting transfers between devices, device_layer(): lax.all_to_all(send_x.reshape(groups, dev_cap, d_model), 'expert', 0, 0,...  4.77 us
  transfers between devices with their start and end apart: 2, of which 2 were waited for; matrix products, arithmetic and copies ran while one was open for 2% of the time, Pallas kernels for 0%

commit v1 on v0

v1 whole, which is shorter than its diff:
```python
import functools

import jax
import jax.numpy as jnp
from jax import lax
from jax.experimental import pallas as pl
from jax.experimental.pallas import tpu as pltpu
from jax.sharding import PartitionSpec as P

MESH = pl.DeviceIdType.MESH
AXIS = "expert"
RIGHT, LEFT = 0, 1


def moe_kernel(
    n_chips,
    tok_hbm, ids_ref, wts_ref, dslot_ref, eslot_ref, wg_hbm, wu_hbm, wd_hbm,
    out_ref,
    xbuf, zbuf, zpart, leafbuf, sumbuf, recvbuf, meta, gate_col, hid, wg, wu, wd,
    load_sem, ag_send, ag_recv, mt_send, mt_recv, xd_send, xd_recv, md_send, md_recv,
    zd_send, zd_recv, lf_send, lf_recv, rs_send, rs_recv,
):
    me = lax.axis_index(AXIS)
    chip, core = me // 2, lax.rem(me, 2)
    mate = chip * 2 + 1 - core
    next_chip = (lax.rem(chip + 1, n_chips), lax.rem(chip + n_chips - 1, n_chips))
    far = n_chips // 2
    last = 2 * far - 1
    n_exp, d_model, d_ff = wg.shape
    half = xbuf.shape[1] // 4
    kind_rows = 2 * half
    sub = half // 2

    def rows(kind, way):
        return pl.ds(pl.multiple_of(kind * kind_rows + way * half, half), half)

    def krows(kind):
        return pl.ds(pl.multiple_of(kind * kind_rows, kind_rows), kind_rows)

    def remote(src, dst, send, recv, to):
        return pltpu.make_async_remote_copy(
            src_ref=src, dst_ref=dst, send_sem=send, recv_sem=recv, device_id={AXIS: to}, device_id_type=MESH
        )

    def ag_copy(step, way, src_i, src_way):
        return remote(
            xbuf.at[src_i, rows(core, src_way)], xbuf.at[step + 1, rows(core, way)],
            ag_send.at[step, way], ag_recv.at[step, way], next_chip[way] * 2 + core,
        )

    def mt_copy(hop, way):
        return remote(
            meta.at[hop, core, way], meta.at[hop + 1, core, way],
            mt_send.at[hop, way], mt_recv.at[hop, way], next_chip[way] * 2 + core,
        )

    def xd_copy(i, kind):
        return remote(xbuf.at[i, krows(kind)], xbuf.at[i, krows(kind)], xd_send.at[i], xd_recv.at[i], mate)

    def md_copy(hop, kind):
        return remote(meta.at[hop, kind], meta.at[hop, kind], md_send.at[hop], md_recv.at[hop], mate)

    def zd_copy(i):
        return remote(zbuf.at[i, krows(1 - core)], zpart.at[i], zd_send.at[i], zd_recv.at[i], mate)

    def leaf_copy(r, way, kind, src_core):
        i, side = (2 * far - 3, 1 - way) if r == 0 else (last, way)
        return remote(
            zbuf.at[i, rows(kind, side)], leafbuf.at[r, way, src_core],
            lf_send.at[r, way, kind], lf_recv.at[r, way, src_core], next_chip[way] * 2 + kind,
        )

    def rs_copy(r, way, s):
        part = pl.ds(s * sub, sub)
        return remote(
            sumbuf.at[r - 2, way, part], recvbuf.at[r - 2, way, part],
            rs_send.at[r - 2, way, s], rs_recv.at[r - 2, way, s], next_chip[way] * 2 + core,
        )

    loads = [
        pltpu.make_async_copy(tok_hbm, xbuf.at[0, krows(core)], load_sem.at[0]),
        pltpu.make_async_copy(wg_hbm, wg, load_sem.at[1]),
        pltpu.make_async_copy(wu_hbm, wu, load_sem.at[2]),
        pltpu.make_async_copy(wd_hbm, wd, load_sem.at[3]),
    ]
    loads[0].start()

    barrier = pltpu.get_barrier_semaphore()
    pl.semaphore_signal(barrier, inc=1, device_id={AXIS: mate}, device_id_type=MESH)
    for way in (RIGHT, LEFT):
        for kind in (0, 1):
            pl.semaphore_signal(barrier, inc=1, device_id={AXIS: next_chip[way] * 2 + kind}, device_id_type=MESH)
    for load in loads[1:]:
        load.start()

    kept = (dslot_ref[...] >= 0) & (eslot_ref[...] >= 0)
    expert = jnp.where(kept, ids_ref[...], -1).astype(jnp.float32)
    table = jnp.concatenate([wts_ref[...], expert], axis=0).astype(jnp.bfloat16)
    for way in (RIGHT, LEFT):
        meta[0, core, way] = table

    pl.semaphore_wait(barrier, 5)
    loads[0].wait()
    for way in (RIGHT, LEFT):
        ag_copy(0, way, 0, way).start()
        mt_copy(0, way).start()
    for way in (RIGHT, LEFT):
        ag_copy(1, way, 0, 1 - way).start()
    md_copy(0, core).start()
    xd_copy(0, core).start()
    for load in loads[1:]:
        load.wait()

    def arrive(i):
        odd = lax.rem(i, 2) == 1
        for way in (RIGHT, LEFT):
            ag_copy(i - 1, way, i, way).wait_recv()

            @pl.when(i <= last - 2)
            def _():
                ag_copy(i + 1, way, i, way).start()

        hop = (i + 1) // 2

        @pl.when(odd)
        def _():
            for way in (RIGHT, LEFT):
                mt_copy(hop - 1, way).wait_recv()

                @pl.when(hop < far)
                def _():
                    mt_copy(hop, way).start()

            md_copy(hop, core).start()

        xd_copy(i, core).start()

    def compute(i):
        hop = (i + 1) // 2
        fresh = (lax.rem(i, 2) == 1) | (i == 0)

        @pl.when(fresh)
        def _():
            md_copy(hop, 1 - core).wait_recv()
            lines = []
            for kind in (0, 1):
                for way in (RIGHT, LEFT):
                    both = meta[hop, kind, way].astype(jnp.float32)
                    top_k = both.shape[0] // 2
                    for e in range(n_exp):
                        mine = both[top_k:] == (me * n_exp + e).astype(jnp.float32)
                        lines.append(jnp.sum(jnp.where(mine, both[:top_k], 0.0), axis=0, keepdims=True))
            stacked = jnp.concatenate(lines, axis=0)
            gate_col[:, : len(lines)] = stacked.T

        xd_copy(i, 1 - core).wait_recv()
        x = xbuf[i]
        blk = 256
        for e in range(n_exp):
            for b in range(d_ff // blk):
                cols = pl.ds(b * blk, blk)
                g = jnp.dot(x, wg[e, :, cols], preferred_element_type=jnp.float32)
                u = jnp.dot(x, wu[e, :, cols], preferred_element_type=jnp.float32)
                hid[e, :, cols] = (jax.nn.silu(g) * u).astype(jnp.bfloat16)
        gates = []
        for e in range(n_exp):
            parts = []
            for kind in (0, 1):
                for way in (RIGHT, LEFT):
                    start = jnp.where(fresh, way, 1 - way) * half
                    col = (kind * 2 + way) * n_exp + e
                    parts.append(gate_col[pl.ds(pl.multiple_of(start, half), half), col : col + 1])
            gates.append(jnp.concatenate(parts, axis=0))
        for b in range(d_model // blk):
            cols = pl.ds(b * blk, blk)
            z = None
            for e in range(n_exp):
                y = jnp.dot(hid[e], wd[e, :, cols], preferred_element_type=jnp.float32)
                y = y.astype(jnp.bfloat16).astype(jnp.float32)
                term = jnp.where(gates[e] != 0.0, gates[e] * y, 0.0)
                z = term if z is None else z + term
            zbuf[i, :, cols] = z.astype(jnp.bfloat16)

    def send_leaf(r):
        for way in (RIGHT, LEFT):
            for kind in (0, 1):
                leaf_copy(r, way, kind, core).start()

    def step(i, carry):
        @pl.when(i <= last - 2)
        def _():
            arrive(i)

        @pl.when(i == last)
        def _():
            arrive(i - 1)
            arrive(i)

        done = i - 1
        compute(done)

        @pl.when(done == last - 2)
        def _():
            send_leaf(0)

        @pl.when(done == last)
        def _():
            send_leaf(1)

        @pl.when((done != last - 2) & (done != last))
        def _():
            zd_copy(done).start()

        return carry

    lax.fori_loop(1, last + 2, step, 0)

    block_of = []
    for r in range(last):
        if r == last - 1:
            block_of.append(2)
        elif r % 2 == 0:
            block_of.append(2 * (far - 1 - r // 2) - 1)
        else:
            block_of.append(last if r == 1 else 2 * (far - r // 2))

    for r in range(2, last):
        i = block_of[r]
        zd_copy(i).wait_recv()
        src = r - 1 if r == last - 1 else r - 2
        for s in range(2):
            for way in (RIGHT, LEFT):
                side = 1 - way
                part = pl.ds(s * sub, sub)
                if src < 2:
                    if s == 0:
                        for kind in (0, 1):
                            leaf_copy(src, way, core, kind).wait_recv()
                    acc = leafbuf[src, way, 0, part].astype(jnp.float32) + leafbuf[src, way, 1, part].astype(jnp.float32)
                else:
                    rs_copy(src, way, s).wait_recv()
                    acc = recvbuf[src - 2, way, part]
                own = pl.ds(pl.multiple_of(core * kind_rows + side * half + s * sub, sub), sub)
                acc = acc + zbuf[i, own, :].astype(jnp.float32)
                acc = acc + zpart[i, pl.ds(side * half + s * sub, sub), :].astype(jnp.float32)
                sumbuf[r - 2, way, part] = acc
                rs_copy(r, way, s).start()

    zd_copy(0).wait_recv()
    for s in range(2):
        for way in (RIGHT, LEFT):
            rs_copy(last - 3, way, s).wait_recv()
    for s in range(2):
        for h in (0, 1):
            part = pl.ds(s * sub, sub)
            rs_copy(last - 1, h, s).wait_recv()
            own = pl.ds(pl.multiple_of(core * kind_rows + h * half + s * sub, sub), sub)
            acc = recvbuf[last - 3, h, part] + recvbuf[last - 5, 1 - h, part]
            acc = acc + zbuf[0, own, :].astype(jnp.float32)
            acc = acc + zpart[0, pl.ds(h * half + s * sub, sub), :].astype(jnp.float32)
            out_ref[pl.ds(h * half + s * sub, sub), :] = acc.astype(out_ref.dtype)

    for way in (RIGHT, LEFT):
        for n in range(last):
            ag_copy(n, way, 0, way).wait_send()
        for hop in range(far):
            mt_copy(hop, way).wait_send()
        for r in (0, 1):
            for kind in (0, 1):
                leaf_copy(r, way, kind, core).wait_send()
        for r in range(2, last):
            for s in range(2):
                rs_copy(r, way, s).wait_send()
    for i in range(last + 1):
        xd_copy(i, core).wait_send()
        if i not in (last - 2, last):
            zd_copy(i).wait_send()
    for hop in range(far + 1):
        md_copy(hop, core).wait_send()


def solution(mesh):
    groups = mesh.shape[AXIS]
    n_chips = groups // 2
    far = n_chips // 2
    last = 2 * far - 1
    row_spec = P(("data", "expert"), None)
    weight_spec = P("expert", None, None)

    def device_layer(tokens, expert_ids, gate_wts, dev_slot, exp_slot, w_gate, w_up, w_down):
        tok_dev, top_k = expert_ids.shape
        d_model = tokens.shape[1]
        e_local, _, d_ff = w_gate.shape
        half = tok_dev // 2
        bf16, f32 = jnp.bfloat16, jnp.float32
        dma = pltpu.SemaphoreType.DMA
        vmem = pl.BlockSpec(memory_space=pltpu.VMEM)
        hbm = pl.BlockSpec(memory_space=pl.ANY)
        return pl.pallas_call(
            functools.partial(moe_kernel, n_chips),
            out_shape=jax.ShapeDtypeStruct((tok_dev, d_model), bf16),
            in_specs=[hbm] + [vmem] * 4 + [hbm] * 3,
            out_specs=vmem,
            scratch_shapes=[
                pltpu.VMEM((last + 1, 4 * half, d_model), bf16),
                pltpu.VMEM((last + 1, 4 * half, d_model), bf16),
                pltpu.VMEM((last + 1, 2 * half, d_model), bf16),
                pltpu.VMEM((2, 2, 2, half, d_model), bf16),
                pltpu.VMEM((last - 2, 2, half, d_model), f32),
                pltpu.VMEM((last - 2, 2, half, d_model), f32),
                pltpu.VMEM((far + 1, 2, 2, 2 * top_k, tok_dev), bf16),
                pltpu.VMEM((tok_dev, 128), f32),
                pltpu.VMEM((e_local, 4 * half, d_ff), bf16),
                pltpu.VMEM(w_gate.shape, bf16),
                pltpu.VMEM(w_up.shape, bf16),
                pltpu.VMEM(w_down.shape, bf16),
                dma((4,)),
                dma((last, 2)), dma((last, 2)),
                dma((far, 2)), dma((far, 2)),
                dma((last + 1,)), dma((last + 1,)),
                dma((far + 1,)), dma((far + 1,)),
                dma((last + 1,)), dma((last + 1,)),
                dma((2, 2, 2)), dma((2, 2, 2)),
                dma((last - 2, 2, 2)), dma((last - 2, 2, 2)),
            ],
            compiler_params=pltpu.CompilerParams(
                collective_id=0, has_side_effects=True, vmem_limit_bytes=56 * 1024 * 1024
            ),
        )(tokens, expert_ids.T, gate_wts.T, dev_slot.T, exp_slot.T, w_gate, w_up, w_down)

    def moe_layer(tokens, expert_ids, gate_wts, dev_slot, exp_slot, w_gate, w_up, w_down):
        mapped = jax.shard_map(device_layer, mesh=mesh, in_specs=(row_spec,) * 5 + (weight_spec,) * 3, out_specs=row_spec, check_vma=False)
        return mapped(tokens, expert_ids, gate_wts, dev_slot, exp_slot, w_gate, w_up, w_down)

    return moe_layer
```

time: 205 us -> 75.7 us (0.37)
  blocking collectives: 79.8 us -> 0 us
  Pallas kernels: 0 us -> 73.9 us
  waiting for transfers between devices: 73.4 us -> 0 us
  matrix products: 32.5 us -> 0 us
  starting transfers between devices: 15.5 us -> 0 us
  other arithmetic: 2.6 us -> 0 us
    all_to_all x1 -> x0, blocking collectives: 79.8 us -> none  [device_layer(): lax.all_to_all(z_rows.reshape(groups, dev_cap, d_model), 'expert', 0, 0,...]
    pallas_call x0 -> x1, Pallas kernels: none -> 73.9 us  [device_layer(): pl.pallas_call(functools.partial(moe_kernel, n_chips), out_shape=jax.Shap...]
    all_to_all x2 -> x0, waiting for transfers between devices: 73.4 us -> none  [the longest x1 70.9 us: device_layer(): lax.all_to_all(send_x.reshape(groups, dev_cap, d_model), 'expert', 0, 0,...]
    dot_general x8 -> x0, matrix products: 32.5 us -> none  [the longest x1 10 us: device_layer(): jnp.einsum('esr,rd->esd', gather_mat, recv_x, preferred_element_type=jnp....]
    all_to_all x2 -> x0, starting transfers between devices: 15.5 us -> none  [the longest x1 10.7 us: device_layer(): lax.all_to_all(send_meta.reshape(groups, dev_cap, e_local, 2), 'expert',...]
  transfers between devices with their start and end apart: 2 -> 0, of which waited for: 2 -> 0; matrix products, arithmetic and copies ran while one was open for 2% -> 0% of each run, Pallas kernels for 0% -> 0%
where the time goes in v1:
time: 75.7 us; the launch traced here: 75.5 us
  Pallas kernels  73.9 us (98%)
  local copies, waits for them, and re-layouts  1.67 us (2%)
    pallas_call x1, Pallas kernels, device_layer(): pl.pallas_call(functools.partial(moe_kernel, n_chips), out_shape=jax.Shap...  73.9 us
    unnamed x1, local copies, waits for them, and re-layouts  1.67 us

profile of v1, /device:TPU:21, one launch (start us, length us, event | category | flops | bytes accessed | tf_op | source)
XLA Modules:
  0.0 75.5 jit_solution(11794668904981325618)
XLA Ops:
  0.0 73.9 %shard_map.82 = bf16[128,1024]{1,0:T(8,128)(2,1)} custom-call(bf16[128,1024]{1,0:T(8,128)(2,1)} %tok_hbm.1, s32[8,128]{1,0:T(8,128)} %bitcast.4, f32[8,128]{1,0:T(8,128)} %bitcast.5, s32[8,128]{1,0:T(8,128)} %bitcast.6, s32[8,128]{1,0:T(8,128)} %bitcast.7, bf16[2,1024,512]{2,1,0:T(8,128)(2,1)} %wg_hbm.1, bf16[2,1024,512]{2,1,0:T(8,128)(2,1)} %wu_hbm.1, ...), custom_call_target="tpu_custom_call" | custom-call | tf_op jit(solution)/shard_map/pallas_call | solution.py:299
  73.9 1.7 %copy.10 = bf16[128,1024]{1,0:T(8,128)(2,1)} copy(bf16[128,1024]{1,0:T(8,128)(2,1)} %shard_map.82) | data formatting | bytes 524288

commit v2 on v1

v2 whole, which is shorter than its diff:
```python
import functools

import jax
import jax.numpy as jnp
from jax import lax
from jax.experimental import pallas as pl
from jax.experimental.pallas import tpu as pltpu
from jax.sharding import PartitionSpec as P

MESH = pl.DeviceIdType.MESH
AXIS = "expert"
RIGHT, LEFT = 0, 1


def moe_kernel(
    n_chips,
    tok_hbm, ids_hbm, wts_hbm, dslot_hbm, eslot_hbm, wg_hbm, wu_hbm, wd_hbm,
    out_ref,
    xbuf, zbuf, zpart, packbuf, leafbuf, sumbuf, recvbuf, meta, gate_col, hid, wg, wu, wd, ids, wts, dslot, eslot,
    load_sem, ag_send, ag_recv, mt_send, mt_recv, xd_send, xd_recv, md_send, md_recv,
    zd_send, zd_recv, lf_send, lf_recv, rs_send, rs_recv,
):
    me = lax.axis_index(AXIS)
    chip, core = me // 2, lax.rem(me, 2)
    mate = chip * 2 + 1 - core
    next_chip = (lax.rem(chip + 1, n_chips), lax.rem(chip + n_chips - 1, n_chips))
    far = n_chips // 2
    last = 2 * far - 1
    n_exp, d_model, d_ff = wg.shape
    n_tok = xbuf.shape[1] // 2
    half = n_tok // 2
    cap = leafbuf.shape[-2]
    wide = d_model // 2
    top_k = ids.shape[0]
    bf16, f32 = jnp.bfloat16, jnp.float32

    def rows(kind, side):
        return pl.ds(pl.multiple_of(kind * n_tok + side * half, half), half)

    def krows(kind):
        return pl.ds(pl.multiple_of(kind * n_tok, n_tok), n_tok)

    def remote(src, dst, send, recv, to):
        return pltpu.make_async_remote_copy(
            src_ref=src, dst_ref=dst, send_sem=send, recv_sem=recv, device_id={AXIS: to}, device_id_type=MESH
        )

    def ag_copy(step, way, src_i, src_side):
        return remote(
            xbuf.at[src_i, rows(core, src_side)], xbuf.at[step + 1, rows(core, way)],
            ag_send.at[step, way], ag_recv.at[step, way], next_chip[way] * 2 + core,
        )

    def mt_copy(hop, way):
        return remote(
            meta.at[hop, core, way], meta.at[hop + 1, core, way],
            mt_send.at[hop, way], mt_recv.at[hop, way], next_chip[way] * 2 + core,
        )

    def xd_copy(i, kind):
        return remote(xbuf.at[i, krows(kind)], xbuf.at[i, krows(kind)], xd_send.at[i], xd_recv.at[i], mate)

    def md_copy(hop, kind):
        return remote(meta.at[hop, kind], meta.at[hop, kind], md_send.at[hop], md_recv.at[hop], mate)

    def zd_copy(i):
        return remote(zbuf.at[i, krows(1 - core)], zpart.at[i], zd_send.at[i], zd_recv.at[i], mate)

    def leaf_copy(r, way, kind, src_core):
        return remote(
            packbuf.at[r, way, kind], leafbuf.at[r, way, src_core],
            lf_send.at[r, way, kind], lf_recv.at[r, way, src_core], next_chip[way] * 2 + kind,
        )

    def n_sub(r):
        return 1 if r < last - 2 else 2

    def rs_copy(r, way, s):
        n = n_tok // n_sub(r)
        part = pl.ds(s * n, n)
        return remote(
            sumbuf.at[r - 2, way, part], recvbuf.at[r - 2, way, part],
            rs_send.at[r - 2, way, s], rs_recv.at[r - 2, way, s], next_chip[way] * 2 + core,
        )

    loads = [
        pltpu.make_async_copy(a, b, load_sem.at[j])
        for j, (a, b) in enumerate(
            (
                (tok_hbm, xbuf.at[0, krows(core)]), (ids_hbm, ids), (wts_hbm, wts), (dslot_hbm, dslot), (eslot_hbm, eslot),
                (wg_hbm, wg), (wu_hbm, wu), (wd_hbm, wd),
            )
        )
    ]
    loads[0].start()
    barrier = pltpu.get_barrier_semaphore()
    pl.semaphore_signal(barrier, inc=1, device_id={AXIS: mate}, device_id_type=MESH)
    for way in (RIGHT, LEFT):
        for kind in (0, 1):
            pl.semaphore_signal(barrier, inc=1, device_id={AXIS: next_chip[way] * 2 + kind}, device_id_type=MESH)
    for load in loads[1:]:
        load.start()
    loads[0].wait()
    pl.semaphore_wait(barrier, 5)

    for way in (RIGHT, LEFT):
        ag_copy(0, way, 0, way).start()
    for load in loads[1:5]:
        load.wait()
    kept = (dslot[...] >= 0) & (eslot[...] >= 0)
    expert = jnp.where(kept, ids[...], -1).astype(f32)
    table = jnp.concatenate([wts[...], expert], axis=0).astype(bf16)
    for way in (RIGHT, LEFT):
        meta[0, core, way] = table
    for way in (RIGHT, LEFT):
        mt_copy(0, way).start()
    for way in (RIGHT, LEFT):
        ag_copy(1, way, 0, 1 - way).start()
    for load in loads[5:]:
        load.wait()

    def experts_of(hop, kind, side):
        return meta[hop, kind, side].astype(f32)[top_k:]

    def routed(expert, device):
        hits = sum(
            jnp.sum((expert == (device * n_exp + e).astype(f32)).astype(f32), axis=0, keepdims=True) for e in range(n_exp)
        )
        return hits > 0.0

    def ranks(masks):
        lines = [m.astype(f32) for m in masks] + [jnp.zeros((8 - len(masks), n_tok), f32)]
        before = lax.broadcasted_iota(jnp.int32, (n_tok, n_tok), 0) < lax.broadcasted_iota(jnp.int32, (n_tok, n_tok), 1)
        return jnp.dot(jnp.concatenate(lines, axis=0).astype(bf16), before.astype(bf16), preferred_element_type=f32)

    def packer(mask, rank):
        place = lax.broadcasted_iota(jnp.int32, (cap, n_tok), 0).astype(f32)
        return jnp.where(mask & (place == rank), 1.0, 0.0)

    def halves(j, side):
        return (2 * j - 1, 2 * j) if side == RIGHT else (2 * j, 2 * j - 1)

    def arrive(i):
        for way in (RIGHT, LEFT):
            ag_copy(i - 1, way, i, way).wait_recv()

            @pl.when(i <= last - 2)
            def _():
                ag_copy(i + 1, way, i, way).start()

        @pl.when(lax.rem(i, 2) == 1)
        def _():
            hop = (i + 1) // 2
            for way in (RIGHT, LEFT):
                mt_copy(hop - 1, way).wait_recv()

                @pl.when(hop < far)
                def _():
                    mt_copy(hop, way).start()

    def compute(i, kind, fresh):
        hop = (i + 1) // 2

        @pl.when(fresh)
        def _():
            lines = []
            for side in (RIGHT, LEFT):
                both = meta[hop, kind, side].astype(f32)
                for e in range(n_exp):
                    mine = both[top_k:] == (me * n_exp + e).astype(f32)
                    lines.append(jnp.sum(jnp.where(mine, both[:top_k], 0.0), axis=0, keepdims=True))
            lines.append(jnp.zeros((8 - len(lines), n_tok), f32))
            gate_col[kind, :, :8] = jnp.concatenate(lines, axis=0).T

        x = xbuf[i, krows(kind)]
        blk = 256
        for e in range(n_exp):
            for b in range(d_ff // blk):
                cols = pl.ds(b * blk, blk)
                g = jnp.dot(x, wg[e, :, cols], preferred_element_type=f32)
                u = jnp.dot(x, wu[e, :, cols], preferred_element_type=f32)
                hid[e, :, cols] = (jax.nn.silu(g) * u).astype(bf16)
        gates = []
        for e in range(n_exp):
            parts = []
            for side in (RIGHT, LEFT):
                start = jnp.where(fresh, side, 1 - side) * half
                col = side * n_exp + e
                parts.append(gate_col[kind, pl.ds(pl.multiple_of(start, half), half), col : col + 1])
            gates.append(jnp.concatenate(parts, axis=0))
        for b in range(d_model // blk):
            cols = pl.ds(b * blk, blk)
            z = None
            for e in range(n_exp):
                y = jnp.dot(hid[e], wd[e, :, cols], preferred_element_type=f32)
                y = y.astype(bf16).astype(f32)
                term = jnp.where(gates[e] != 0.0, gates[e] * y, 0.0)
                z = term if z is None else z + term
            zbuf[i, krows(kind), cols] = z.astype(bf16)

    def send_leaf(r, kind):
        if r == 0:
            masks = [routed(experts_of(far - 1, kind, 1 - way), me) for way in (RIGHT, LEFT)]
        else:
            masks = [routed(experts_of(far, kind, RIGHT), me)]
        rank = ranks(masks)
        for way in (RIGHT, LEFT):
            if r == 0:
                n, side, h = way, 1 - way, 1 - way
                places = [(i, side) for i in halves(far - 1, side)]
            else:
                n, h = 0, way
                places = [(last, RIGHT), (last, LEFT)]
            pick = packer(masks[n], rank[n : n + 1]).astype(bf16)
            cols = pl.ds(h * wide, wide)
            z = jnp.concatenate([zbuf[i, rows(kind, side), cols] for i, side in places], axis=0)
            packbuf[r, way, kind] = jnp.dot(pick, z, preferred_element_type=f32).astype(bf16)
            leaf_copy(r, way, kind, core).start()

    def step(i, carry):
        odd = lax.rem(i, 2) == 1
        fresh = odd | (i == 0)

        @pl.when(i >= 1)
        def _():
            arrive(i)

        xd_copy(i, core).start()

        @pl.when(fresh)
        def _():
            md_copy((i + 1) // 2, core).start()

        def one_kind(turn, carry):
            kind = lax.rem(core + turn, 2)

            @pl.when(turn == 1)
            def _():
                xd_copy(i, 1 - core).wait_recv()

                @pl.when(fresh)
                def _():
                    md_copy((i + 1) // 2, 1 - core).wait_recv()

            compute(i, kind, fresh)

            @pl.when(i == last - 1)
            def _():
                send_leaf(0, kind)

            @pl.when(i == last)
            def _():
                send_leaf(1, kind)

            return carry

        lax.fori_loop(0, 2, one_kind, 0)

        @pl.when(i < last)
        def _():
            zd_copy(i).start()

        return carry

    lax.fori_loop(0, last + 1, step, 0)

    def plan(r, way):
        if r == last - 1:
            return 1, way
        return (far - 1 - r // 2, 1 - way) if r % 2 == 0 else (far - r // 2, way)

    def unpack(r, way):
        j, _ = plan(r, way)
        expert = experts_of(j - 1, core, 1 - way)
        masks = [routed(expert, next_chip[1 - way] * 2 + k) for k in (0, 1)]
        rank = ranks(masks)
        picks = [packer(masks[k], rank[k : k + 1]).T.astype(bf16) for k in (0, 1)]
        for k in (0, 1):
            leaf_copy(r, way, core, k).wait_recv()
        return sum(jnp.dot(picks[k], leafbuf[r, way, k], preferred_element_type=f32) for k in (0, 1))

    known = set()
    for r in range(2, last):
        src = r - 1 if r == last - 1 else r - 2
        for i in halves(plan(r, RIGHT)[0], RIGHT):
            if i not in known:
                known.add(i)
                zd_copy(i).wait_recv()
        for t in (0, 1):
            for way in (RIGHT, LEFT):
                j, h = plan(r, way)
                side = 1 - way
                i = halves(j, side)[t]
                part, cols = pl.ds(t * half, half), pl.ds(h * wide, wide)
                if src < 2:
                    if t == 0:
                        sumbuf[r - 2, way] = unpack(src, way)
                    acc = sumbuf[r - 2, way, part]
                else:
                    if t < n_sub(src):
                        rs_copy(src, way, t).wait_recv()
                    acc = recvbuf[src - 2, way, part]
                acc = acc + zbuf[i, rows(core, side), cols].astype(f32)
                acc = acc + zpart[i, pl.ds(side * half, half), cols].astype(f32)
                sumbuf[r - 2, way, part] = acc
                if n_sub(r) == 2:
                    rs_copy(r, way, t).start()
                elif t == 1:
                    rs_copy(r, way, 0).start()

    zd_copy(0).wait_recv()
    for way in (RIGHT, LEFT):
        rs_copy(last - 3, way, 0).wait_recv()
    for t in (0, 1):
        for way in (RIGHT, LEFT):
            part, cols = pl.ds(t * half, half), pl.ds(way * wide, wide)
            rs_copy(last - 1, way, t).wait_recv()
            acc = recvbuf[last - 3, way, part] + recvbuf[last - 5, 1 - way, part]
            acc = acc + zbuf[0, rows(core, t), cols].astype(f32)
            acc = acc + zpart[0, part, cols].astype(f32)
            out_ref[part, cols] = acc.astype(out_ref.dtype)

    for way in (RIGHT, LEFT):
        for n in range(last):
            ag_copy(n, way, 0, way).wait_send()
        for hop in range(far):
            mt_copy(hop, way).wait_send()
        for r in (0, 1):
            for kind in (0, 1):
                leaf_copy(r, way, kind, core).wait_send()
        for r in range(2, last):
            for s in range(n_sub(r)):
                rs_copy(r, way, s).wait_send()
    for i in range(last + 1):
        xd_copy(i, core).wait_send()
        if i < last:
            zd_copy(i).wait_send()
    for hop in range(far + 1):
        md_copy(hop, core).wait_send()


def solution(mesh):
    groups = mesh.shape[AXIS]
    n_chips = groups // 2
    far = n_chips // 2
    last = 2 * far - 1
    row_spec = P(("data", "expert"), None)
    weight_spec = P("expert", None, None)

    def device_layer(tokens, expert_ids, gate_wts, dev_slot, exp_slot, w_gate, w_up, w_down):
        tok_dev, top_k = expert_ids.shape
        d_model = tokens.shape[1]
        e_local, _, d_ff = w_gate.shape
        dev_cap = min(tok_dev, 8 * ((3 * tok_dev * top_k + 16 * groups - 1) // (16 * groups)))
        bf16, f32, i32 = jnp.bfloat16, jnp.float32, jnp.int32
        dma = pltpu.SemaphoreType.DMA
        args = (tokens, expert_ids.T, gate_wts.T, dev_slot.T, exp_slot.T, w_gate, w_up, w_down)
        args = [pltpu.with_memory_space_constraint(a, pltpu.HBM) for a in args]
        return pl.pallas_call(
            functools.partial(moe_kernel, n_chips),
            out_shape=jax.ShapeDtypeStruct((tok_dev, d_model), bf16),
            in_specs=[pl.BlockSpec(memory_space=pltpu.HBM)] * len(args),
            out_specs=pl.BlockSpec(memory_space=pltpu.VMEM),
            scratch_shapes=[
                pltpu.VMEM((last + 1, 2 * tok_dev, d_model), bf16),
                pltpu.VMEM((last + 1, 2 * tok_dev, d_model), bf16),
                pltpu.VMEM((last, tok_dev, d_model), bf16),
                pltpu.VMEM((2, 2, 2, dev_cap, d_model // 2), bf16),
                pltpu.VMEM((2, 2, 2, dev_cap, d_model // 2), bf16),
                pltpu.VMEM((last - 2, 2, tok_dev, d_model // 2), f32),
                pltpu.VMEM((last - 2, 2, tok_dev, d_model // 2), f32),
                pltpu.VMEM((far + 1, 2, 2, 2 * top_k, tok_dev), bf16),
                pltpu.VMEM((2, tok_dev, 128), f32),
                pltpu.VMEM((e_local, tok_dev, d_ff), bf16),
                pltpu.VMEM(w_gate.shape, bf16),
                pltpu.VMEM(w_up.shape, bf16),
                pltpu.VMEM(w_down.shape, bf16),
                pltpu.VMEM((top_k, tok_dev), i32),
                pltpu.VMEM((top_k, tok_dev), f32),
                pltpu.VMEM((top_k, tok_dev), i32),
                pltpu.VMEM((top_k, tok_dev), i32),
                dma((8,)),
                dma((last, 2)), dma((last, 2)),
                dma((far, 2)), dma((far, 2)),
                dma((last + 1,)), dma((last + 1,)),
                dma((far + 1,)), dma((far + 1,)),
                dma((last,)), dma((last,)),
                dma((2, 2, 2)), dma((2, 2, 2)),
                dma((last - 2, 2, 2)), dma((last - 2, 2, 2)),
            ],
            compiler_params=pltpu.CompilerParams(
                collective_id=0, has_side_effects=True, vmem_limit_bytes=48 * 1024 * 1024
            ),
        )(*args)

    def moe_layer(tokens, expert_ids, gate_wts, dev_slot, exp_slot, w_gate, w_up, w_down):
        mapped = jax.shard_map(device_layer, mesh=mesh, in_specs=(row_spec,) * 5 + (weight_spec,) * 3, out_specs=row_spec, check_vma=False)
        return mapped(tokens, expert_ids, gate_wts, dev_slot, exp_slot, w_gate, w_up, w_down)

    return moe_layer
```

time: 75.7 us -> 70.7 us (0.934)
  Pallas kernels: 73.9 us -> 69.9 us
  local copies, waits for them, and re-layouts: 1.67 us -> 0.71 us
    pallas_call x1, Pallas kernels: 73.9 us -> 69.9 us  [device_layer(): pl.pallas_call(functools.partial(moe_kernel, n_chips), out_shape=jax.Shap...]
    unnamed x1, local copies, waits for them, and re-layouts: 1.67 us -> 0.71 us
where the time goes in v2:
time: 70.7 us; the launch traced here: 70.6 us
  Pallas kernels  69.9 us (99%)
  local copies, waits for them, and re-layouts  0.71 us (1%)
    pallas_call x1, Pallas kernels, device_layer(): pl.pallas_call(functools.partial(moe_kernel, n_chips), out_shape=jax.Shap...  69.9 us

profile of v2, /device:TPU:21, one launch (start us, length us, event | category | flops | bytes accessed | tf_op | source)
XLA Modules:
  0.0 70.6 jit_solution(3813959117619162203)
XLA Ops:
  0.0 69.9 %shard_map.82 = bf16[128,1024]{1,0:T(8,128)(2,1)S(1)} custom-call(bf16[128,1024]{1,0:T(8,128)(2,1)} %tok_hbm.1, s32[8,128]{1,0:T(8,128)} %bitcast.4, f32[8,128]{1,0:T(8,128)} %bitcast.5, s32[8,128]{1,0:T(8,128)} %bitcast.6, s32[8,128]{1,0:T(8,128)} %bitcast.7, bf16[2,1024,512]{2,1,0:T(8,128)(2,1)} %wg_hbm.1, bf16[2,1024,512]{2,1,0:T(8,128)(2,1)} %wu_hbm.1, ...), custom_call_target="tpu_custom_call" | custom-call | tf_op jit(solution)/shard_map/pallas_call | solution.py:359
  69.9 0.7 copy.10

commit v3 on v2

--- a/solution.py
+++ b/solution.py
@@ -16,7 +16,7 @@
     n_chips,
     tok_hbm, ids_hbm, wts_hbm, dslot_hbm, eslot_hbm, wg_hbm, wu_hbm, wd_hbm,
     out_ref,
-    xbuf, zbuf, zpart, packbuf, leafbuf, sumbuf, recvbuf, meta, gate_col, hid, wg, wu, wd, ids, wts, dslot, eslot,
+    xbuf, zbuf, zpart, packbuf, leafbuf, sumbuf, recvbuf, meta, gate_col, picks, hid, w_in, wd, ids, wts, dslot, eslot,
     load_sem, ag_send, ag_recv, mt_send, mt_recv, xd_send, xd_recv, md_send, md_recv,
     zd_send, zd_recv, lf_send, lf_recv, rs_send, rs_recv,
 ):
@@ -26,7 +26,7 @@
     next_chip = (lax.rem(chip + 1, n_chips), lax.rem(chip + n_chips - 1, n_chips))
     far = n_chips // 2
     last = 2 * far - 1
-    n_exp, d_model, d_ff = wg.shape
+    _, n_exp, d_model, d_ff = w_in.shape
     n_tok = xbuf.shape[1] // 2
     half = n_tok // 2
     cap = leafbuf.shape[-2]
@@ -48,48 +48,55 @@
     def ag_copy(step, way, src_i, src_side):
         return remote(
             xbuf.at[src_i, rows(core, src_side)], xbuf.at[step + 1, rows(core, way)],
-            ag_send.at[step, way], ag_recv.at[step, way], next_chip[way] * 2 + core,
+            ag_send, ag_recv.at[step, way], next_chip[way] * 2 + core,
         )
 
     def mt_copy(hop, way):
         return remote(
             meta.at[hop, core, way], meta.at[hop + 1, core, way],
-            mt_send.at[hop, way], mt_recv.at[hop, way], next_chip[way] * 2 + core,
+            mt_send, mt_recv.at[hop], next_chip[way] * 2 + core,
         )
 
     def xd_copy(i, kind):
-        return remote(xbuf.at[i, krows(kind)], xbuf.at[i, krows(kind)], xd_send.at[i], xd_recv.at[i], mate)
+        return remote(xbuf.at[i, krows(kind)], xbuf.at[i, krows(kind)], xd_send, xd_recv.at[i], mate)
 
     def md_copy(hop, kind):
-        return remote(meta.at[hop, kind], meta.at[hop, kind], md_send.at[hop], md_recv.at[hop], mate)
+        return remote(meta.at[hop, kind], meta.at[hop, kind], md_send, md_recv.at[hop], mate)
 
     def zd_copy(i):
-        return remote(zbuf.at[i, krows(1 - core)], zpart.at[i], zd_send.at[i], zd_recv.at[i], mate)
+        return remote(zbuf.at[i, krows(1 - core)], zpart.at[i], zd_send, zd_recv, mate)
 
     def leaf_copy(r, way, kind, src_core):
         return remote(
             packbuf.at[r, way, kind], leafbuf.at[r, way, src_core],
-            lf_send.at[r, way, kind], lf_recv.at[r, way, src_core], next_chip[way] * 2 + kind,
+            lf_send, lf_recv.at[r, way], next_chip[way] * 2 + kind,
         )
 
     def n_sub(r):
         return 1 if r < last - 2 else 2
+
+    def rs_slot(r, way, s):
+        if n_sub(r) == 1:
+            return r - 2
+        return last - 4 + (r - last + 2) * 4 + s * 2 + way
 
     def rs_copy(r, way, s):
         n = n_tok // n_sub(r)
         part = pl.ds(s * n, n)
         return remote(
             sumbuf.at[r - 2, way, part], recvbuf.at[r - 2, way, part],
-            rs_send.at[r - 2, way, s], rs_recv.at[r - 2, way, s], next_chip[way] * 2 + core,
-        )
+            rs_send, rs_recv.at[rs_slot(r, way, s)], next_chip[way] * 2 + core,
+        )
+
+    def drain(ref, sem):
+        pltpu.make_async_copy(ref, ref, sem).wait()
 
     loads = [
         pltpu.make_async_copy(a, b, load_sem.at[j])
-        for j, (a, b) in enumerate(
-            (
-                (tok_hbm, xbuf.at[0, krows(core)]), (ids_hbm, ids), (wts_hbm, wts), (dslot_hbm, dslot), (eslot_hbm, eslot),
-                (wg_hbm, wg), (wu_hbm, wu), (wd_hbm, wd),
-            )
+        for a, b, j in (
+            (tok_hbm, xbuf.at[0, krows(core)], 0),
+            (ids_hbm, ids, 1), (wts_hbm, wts, 1), (dslot_hbm, dslot, 1), (eslot_hbm, eslot, 1),
+            (wg_hbm, w_in.at[0], 2), (wu_hbm, w_in.at[1], 2), (wd_hbm, wd, 3),
         )
     ]
     loads[0].start()
@@ -105,8 +112,7 @@
 
     for way in (RIGHT, LEFT):
         ag_copy(0, way, 0, way).start()
-    for load in loads[1:5]:
-        load.wait()
+    drain(gate_col.at[0, : 4 * top_k], load_sem.at[1])
     kept = (dslot[...] >= 0) & (eslot[...] >= 0)
     expert = jnp.where(kept, ids[...], -1).astype(f32)
     table = jnp.concatenate([wts[...], expert], axis=0).astype(bf16)
@@ -116,8 +122,8 @@
         mt_copy(0, way).start()
     for way in (RIGHT, LEFT):
         ag_copy(1, way, 0, 1 - way).start()
-    for load in loads[5:]:
-        load.wait()
+    drain(w_in, load_sem.at[2])
+    loads[7].wait()
 
     def experts_of(hop, kind, side):
         return meta[hop, kind, side].astype(f32)[top_k:]
@@ -151,11 +157,11 @@
         @pl.when(lax.rem(i, 2) == 1)
         def _():
             hop = (i + 1) // 2
-            for way in (RIGHT, LEFT):
-                mt_copy(hop - 1, way).wait_recv()
-
-                @pl.when(hop < far)
-                def _():
+            drain(meta.at[hop, core], mt_recv.at[hop - 1])
+
+            @pl.when(hop < far)
+            def _():
+                for way in (RIGHT, LEFT):
                     mt_copy(hop, way).start()
 
     def compute(i, kind, fresh):
@@ -177,8 +183,8 @@
         for e in range(n_exp):
             for b in range(d_ff // blk):
                 cols = pl.ds(b * blk, blk)
-                g = jnp.dot(x, wg[e, :, cols], preferred_element_type=f32)
-                u = jnp.dot(x, wu[e, :, cols], preferred_element_type=f32)
+                g = jnp.dot(x, w_in[0, e, :, cols], preferred_element_type=f32)
+                u = jnp.dot(x, w_in[1, e, :, cols], preferred_element_type=f32)
                 hid[e, :, cols] = (jax.nn.silu(g) * u).astype(bf16)
         gates = []
         for e in range(n_exp):
@@ -198,23 +204,26 @@
                 z = term if z is None else z + term
             zbuf[i, krows(kind), cols] = z.astype(bf16)
 
-    def send_leaf(r, kind):
+    def prepare(r, kind):
         if r == 0:
             masks = [routed(experts_of(far - 1, kind, 1 - way), me) for way in (RIGHT, LEFT)]
         else:
-            masks = [routed(experts_of(far, kind, RIGHT), me)]
+            masks = [routed(experts_of(far, kind, RIGHT), me)] * 2
         rank = ranks(masks)
         for way in (RIGHT, LEFT):
+            picks[kind, way] = packer(masks[way], rank[way : way + 1]).astype(bf16)
+
+    def send_leaf(r, kind):
+        for way in (RIGHT, LEFT):
             if r == 0:
-                n, side, h = way, 1 - way, 1 - way
+                side, h = 1 - way, 1 - way
                 places = [(i, side) for i in halves(far - 1, side)]
             else:
-                n, h = 0, way
+                h = way
                 places = [(last, RIGHT), (last, LEFT)]
-            pick = packer(masks[n], rank[n : n + 1]).astype(bf16)
             cols = pl.ds(h * wide, wide)
             z = jnp.concatenate([zbuf[i, rows(kind, side), cols] for i, side in places], axis=0)
-            packbuf[r, way, kind] = jnp.dot(pick, z, preferred_element_type=f32).astype(bf16)
+            packbuf[r, way, kind] = jnp.dot(picks[kind, way], z, preferred_element_type=f32).astype(bf16)
             leaf_copy(r, way, kind, core).start()
 
     def step(i, carry):
@@ -242,7 +251,15 @@
                 def _():
                     md_copy((i + 1) // 2, 1 - core).wait_recv()
 
+            @pl.when(i == last)
+            def _():
+                prepare(1, kind)
+
             compute(i, kind, fresh)
+
+            @pl.when(i == last - 2)
+            def _():
+                prepare(0, kind)
 
             @pl.when(i == last - 1)
             def _():
@@ -275,17 +292,14 @@
         masks = [routed(expert, next_chip[1 - way] * 2 + k) for k in (0, 1)]
         rank = ranks(masks)
         picks = [packer(masks[k], rank[k : k + 1]).T.astype(bf16) for k in (0, 1)]
-        for k in (0, 1):
-            leaf_copy(r, way, core, k).wait_recv()
+        drain(leafbuf.at[r, way], lf_recv.at[r, way])
         return sum(jnp.dot(picks[k], leafbuf[r, way, k], preferred_element_type=f32) for k in (0, 1))
 
-    known = set()
+    drain(zpart, zd_recv)
     for r in range(2, last):
         src = r - 1 if r == last - 1 else r - 2
-        for i in halves(plan(r, RIGHT)[0], RIGHT):
-            if i not in known:
-                known.add(i)
-                zd_copy(i).wait_recv()
+        if 2 <= src < last - 2:
+            drain(recvbuf.at[src - 2], rs_recv.at[src - 2])
         for t in (0, 1):
             for way in (RIGHT, LEFT):
                 j, h = plan(r, way)
@@ -297,7 +311,7 @@
                         sumbuf[r - 2, way] = unpack(src, way)
                     acc = sumbuf[r - 2, way, part]
                 else:
-                    if t < n_sub(src):
+                    if n_sub(src) == 2:
                         rs_copy(src, way, t).wait_recv()
                     acc = recvbuf[src - 2, way, part]
                 acc = acc + zbuf[i, rows(core, side), cols].astype(f32)
@@ -308,9 +322,7 @@
                 elif t == 1:
                     rs_copy(r, way, 0).start()
 
-    zd_copy(0).wait_recv()
-    for way in (RIGHT, LEFT):
-        rs_copy(last - 3, way, 0).wait_recv()
+    drain(recvbuf.at[last - 5], rs_recv.at[last - 5])
     for t in (0, 1):
         for way in (RIGHT, LEFT):
             part, cols = pl.ds(t * half, half), pl.ds(way * wide, wide)
@@ -320,23 +332,13 @@
             acc = acc + zpart[0, part, cols].astype(f32)
             out_ref[part, cols] = acc.astype(out_ref.dtype)
 
-    for way in (RIGHT, LEFT):
-        for n in range(last):
-            ag_copy(n, way, 0, way).wait_send()
-        for hop in range(far):
-            mt_copy(hop, way).wait_send()
-        for r in (0, 1):
-            for kind in (0, 1):
-                leaf_copy(r, way, kind, core).wait_send()
-        for r in range(2, last):
-            for s in range(n_sub(r)):
-                rs_copy(r, way, s).wait_send()
-    for i in range(last + 1):
-        xd_copy(i, core).wait_send()
-        if i < last:
-            zd_copy(i).wait_send()
-    for hop in range(far + 1):
-        md_copy(hop, core).wait_send()
+    drain(xbuf.at[1:, :n_tok], ag_send)
+    drain(meta.at[:far, 0], mt_send)
+    drain(xbuf.at[:, :n_tok], xd_send)
+    drain(meta.at[:, 0], md_send)
+    drain(zpart, zd_send)
+    drain(packbuf, lf_send)
+    drain(sumbuf, rs_send)
 
 
 def solution(mesh):
@@ -371,22 +373,22 @@
                 pltpu.VMEM((last - 2, 2, tok_dev, d_model // 2), f32),
                 pltpu.VMEM((far + 1, 2, 2, 2 * top_k, tok_dev), bf16),
                 pltpu.VMEM((2, tok_dev, 128), f32),
+                pltpu.VMEM((2, 2, dev_cap, tok_dev), bf16),
                 pltpu.VMEM((e_local, tok_dev, d_ff), bf16),
-                pltpu.VMEM(w_gate.shape, bf16),
-                pltpu.VMEM(w_up.shape, bf16),
+                pltpu.VMEM((2, *w_gate.shape), bf16),
                 pltpu.VMEM(w_down.shape, bf16),
                 pltpu.VMEM((top_k, tok_dev), i32),
                 pltpu.VMEM((top_k, tok_dev), f32),
                 pltpu.VMEM((top_k, tok_dev), i32),
                 pltpu.VMEM((top_k, tok_dev), i32),
-                dma((8,)),
-                dma((last, 2)), dma((last, 2)),
-                dma((far, 2)), dma((far, 2)),
-                dma((last + 1,)), dma((last + 1,)),
-                dma((far + 1,)), dma((far + 1,)),
-                dma((last,)), dma((last,)),
-                dma((2, 2, 2)), dma((2, 2, 2)),
-                dma((last - 2, 2, 2)), dma((last - 2, 2, 2)),
+                dma((4,)),
+                dma, dma((last, 2)),
+                dma, dma((far,)),
+                dma, dma((last + 1,)),
+                dma, dma((far + 1,)),
+                dma, dma,
+                dma, dma((2, 2)),
+                dma, dma((last + 4,)),
             ],
             compiler_params=pltpu.CompilerParams(
                 collective_id=0, has_side_effects=True, vmem_limit_bytes=48 * 1024 * 1024

time: 70.7 us -> 69.8 us (0.987)
  Pallas kernels: 69.9 us -> 69 us
    pallas_call x1, Pallas kernels: 69.9 us -> 69 us  [device_layer(): pl.pallas_call(functools.partial(moe_kernel, n_chips), out_shape=jax.Shap...]
where the time goes in v3:
time: 69.8 us; the launch traced here: 69.7 us
  Pallas kernels  69 us (99%)
  local copies, waits for them, and re-layouts  0.71 us (1%)
    pallas_call x1, Pallas kernels, device_layer(): pl.pallas_call(functools.partial(moe_kernel, n_chips), out_shape=jax.Shap...  69 us

profile of v3, /device:TPU:21, one launch (start us, length us, event | category | flops | bytes accessed | tf_op | source)
XLA Modules:
  0.0 69.7 jit_solution(7400259947122970095)
XLA Ops:
  0.0 69.0 %shard_map.82 = bf16[128,1024]{1,0:T(8,128)(2,1)S(1)} custom-call(bf16[128,1024]{1,0:T(8,128)(2,1)} %tok_hbm.1, s32[8,128]{1,0:T(8,128)} %bitcast.4, f32[8,128]{1,0:T(8,128)} %bitcast.5, s32[8,128]{1,0:T(8,128)} %bitcast.6, s32[8,128]{1,0:T(8,128)} %bitcast.7, bf16[2,1024,512]{2,1,0:T(8,128)(2,1)} %wg_hbm.1, bf16[2,1024,512]{2,1,0:T(8,128)(2,1)} %wu_hbm.1, ...), custom_call_target="tpu_custom_call" | custom-call | tf_op jit(solution)/shard_map/pallas_call | solution.py:361
  69.0 0.7 %copy.10 = bf16[128,1024]{1,0:T(8,128)(2,1)} copy(bf16[128,1024]{1,0:T(8,128)(2,1)S(1)} %shard_map.82) | data formatting | bytes 524288

commit v4 on v3

v4 whole, which is shorter than its diff:
```python
import functools

import jax
import jax.numpy as jnp
from jax import lax
from jax.experimental import pallas as pl
from jax.experimental.pallas import tpu as pltpu
from jax.sharding import PartitionSpec as P

MESH = pl.DeviceIdType.MESH
AXIS = "expert"
RIGHT, LEFT = 0, 1


def chain_order(far):
    a, b, c, d = far + 1, far - 1, far, far - 2
    assert d == 2
    return [
(d, 2), (b, 3), (a, 5), (c, 4), (b, 2), (a, 4), (c, 3), (b, 1), (a, 3), (c, 2), (a, 2), (d, 1), (c, 1), (a, 1),
    ]


def moe_kernel(
    n_chips,
    tok_hbm, ids_hbm, wts_hbm, dslot_hbm, eslot_hbm, wg_hbm, wu_hbm, wd_hbm,
    out_ref,
    xbuf, zbuf, zpart, packbuf, leafbuf, sumbuf, recvbuf, meta, gate_col, picks, hid, w_in, wd, ids, wts, dslot, eslot,
    load_sem, ag_send, ag_recv, mt_send, mt_recv, xd_send, xd_recv, md_send, md_recv,
    zd_send, zd_recv, lf_send, lf_recv, rs_send, rs_recv,
):
    me = lax.axis_index(AXIS)
    chip, core = me // 2, lax.rem(me, 2)
    mate = chip * 2 + 1 - core
    next_chip = (lax.rem(chip + 1, n_chips), lax.rem(chip + n_chips - 1, n_chips))
    far = n_chips // 2
    last = 2 * far - 1
    _, n_exp, d_model, d_ff = w_in.shape
    n_tok = xbuf.shape[1] // 2
    quarter = n_tok // 4
    cap = leafbuf.shape[-2]
    wide = d_model // 4
    top_k = ids.shape[0]
    bf16, f32 = jnp.bfloat16, jnp.float32
    sends = chain_order(far)
    n_leaf = 4

    def rows(kind, part, side):
        return pl.ds(pl.multiple_of(kind * n_tok + part * 2 * quarter + side * quarter, quarter), quarter)

    def both_sides(kind, part):
        return pl.ds(pl.multiple_of(kind * n_tok + part * 2 * quarter, 2 * quarter), 2 * quarter)

    def krows(kind):
        return pl.ds(pl.multiple_of(kind * n_tok, n_tok), n_tok)

    def remote(src, dst, send, recv, to):
        return pltpu.make_async_remote_copy(
            src_ref=src, dst_ref=dst, send_sem=send, recv_sem=recv, device_id={AXIS: to}, device_id_type=MESH
        )

    def ag_copy(step, way, part, src_i, src_side):
        return remote(
            xbuf.at[src_i, rows(core, part, src_side)], xbuf.at[step + 1, rows(core, part, way)],
            ag_send, ag_recv.at[step, part], next_chip[way] * 2 + core,
        )

    def mt_copy(hop, way):
        return remote(
            meta.at[hop, core, way], meta.at[hop + 1, core, way],
            mt_send, mt_recv.at[hop], next_chip[way] * 2 + core,
        )

    def xd_copy(i, kind):
        return remote(xbuf.at[i, krows(kind)], xbuf.at[i, krows(kind)], xd_send, xd_recv.at[i], mate)

    def md_copy(hop, kind):
        return remote(meta.at[hop, kind], meta.at[hop, kind], md_send, md_recv.at[hop], mate)

    def zd_copy(i):
        return remote(zbuf.at[i, krows(1 - core)], zpart.at[i], zd_send, zd_recv.at[i // last], mate)

    def group_of(length, way):
        order = (far, far - 1, far + 1, far - 2)
        return order.index(length if way == RIGHT else n_chips - 1 - length)

    def leaf_copy(n, way, kind):
        return remote(
            packbuf.at[n, way, kind], leafbuf.at[n, way, core], lf_send, lf_recv.at[n], next_chip[way] * 2 + kind
        )

    def rs_copy(n, way):
        return remote(
            sumbuf.at[n - n_leaf, way], recvbuf.at[n - n_leaf, way], rs_send, rs_recv.at[n - n_leaf], next_chip[way] * 2 + core
        )

    def drain(ref, sem):
        pltpu.make_async_copy(ref, ref, sem).wait()

    loads = [
        pltpu.make_async_copy(a, b, load_sem.at[j])
        for a, b, j in (
            (tok_hbm, xbuf.at[0, krows(core)], 0),
            (ids_hbm, ids, 1), (wts_hbm, wts, 1), (dslot_hbm, dslot, 1), (eslot_hbm, eslot, 1),
            (wg_hbm, w_in.at[0], 2), (wu_hbm, w_in.at[1], 2), (wd_hbm, wd, 3),
        )
    ]
    loads[0].start()
    barrier = pltpu.get_barrier_semaphore()
    pl.semaphore_signal(barrier, inc=1, device_id={AXIS: mate}, device_id_type=MESH)
    for way in (RIGHT, LEFT):
        for kind in (0, 1):
            pl.semaphore_signal(barrier, inc=1, device_id={AXIS: next_chip[way] * 2 + kind}, device_id_type=MESH)
    for load in loads[1:]:
        load.start()
    loads[0].wait()
    pl.semaphore_wait(barrier, 5)

    for part in (0, 1):
        for way in (RIGHT, LEFT):
            ag_copy(0, way, part, 0, way).start()
    drain(gate_col.at[0, : 4 * top_k], load_sem.at[1])
    kept = (dslot[...] >= 0) & (eslot[...] >= 0)
    expert = jnp.where(kept, ids[...], -1).astype(f32)
    table = jnp.concatenate([wts[...], expert], axis=0).astype(bf16)
    for way in (RIGHT, LEFT):
        meta[0, core, way] = table
    for way in (RIGHT, LEFT):
        mt_copy(0, way).start()
    for part in (0, 1):
        for way in (RIGHT, LEFT):
            ag_copy(1, way, part, 0, 1 - way).start()
    drain(w_in, load_sem.at[2])
    loads[7].wait()

    def experts_of(hop, kind, side):
        return meta[hop, kind, side].astype(f32)[top_k:]

    def routed(expert, device):
        hits = sum(
            jnp.sum((expert == (device * n_exp + e).astype(f32)).astype(f32), axis=0, keepdims=True) for e in range(n_exp)
        )
        return hits > 0.0

    def ranks(masks):
        lines = [m.astype(f32) for m in masks] + [jnp.zeros((8 - len(masks), n_tok), f32)]
        before = lax.broadcasted_iota(jnp.int32, (n_tok, n_tok), 0) < lax.broadcasted_iota(jnp.int32, (n_tok, n_tok), 1)
        return jnp.dot(jnp.concatenate(lines, axis=0).astype(bf16), before.astype(bf16), preferred_element_type=f32)

    def packer(mask, rank):
        place = lax.broadcasted_iota(jnp.int32, (cap, n_tok), 0).astype(f32)
        return jnp.where(mask & (place == rank), 1.0, 0.0)

    def place(ahead, way):
        if ahead in (0, far):
            return [(0 if ahead == 0 else last, part, side) for part in (0, 1) for side in (RIGHT, LEFT)]
        side, hop = (1 - way, ahead) if ahead < far else (way, n_chips - ahead)
        return [(2 * hop - 1 if side == h else 2 * hop, part, side) for part in (0, 1) for h in (0, 1)]

    def experts_ahead(ahead, way, kind):
        if ahead == far:
            return experts_of(far, kind, RIGHT)
        return experts_of(ahead, kind, 1 - way) if ahead < far else experts_of(n_chips - ahead, kind, way)

    def arrive(i, part):
        drain(xbuf.at[i, both_sides(core, part)], ag_recv.at[i - 1, part])

        @pl.when(i <= last - 2)
        def _():
            for way in (RIGHT, LEFT):
                ag_copy(i + 1, way, part, i, way).start()

        if part == 1:

            @pl.when(lax.rem(i, 2) == 1)
            def _():
                hop = (i + 1) // 2
                drain(meta.at[hop, core], mt_recv.at[hop - 1])

                @pl.when(hop < far)
                def _():
                    for way in (RIGHT, LEFT):
                        mt_copy(hop, way).start()

    def compute(i, kind):
        hop = (i + 1) // 2
        fresh = (lax.rem(i, 2) == 1) | (i == 0)

        @pl.when(fresh)
        def _():
            lines = []
            for side in (RIGHT, LEFT):
                both = meta[hop, kind, side].astype(f32)
                for e in range(n_exp):
                    mine = both[top_k:] == (me * n_exp + e).astype(f32)
                    lines.append(jnp.sum(jnp.where(mine, both[:top_k], 0.0), axis=0, keepdims=True))
            lines.append(jnp.zeros((8 - len(lines), n_tok), f32))
            gate_col[kind, :, :8] = jnp.concatenate(lines, axis=0).T

        x = xbuf[i, krows(kind)]
        blk = 256
        for e in range(n_exp):
            for b in range(d_ff // blk):
                cols = pl.ds(b * blk, blk)
                g = jnp.dot(x, w_in[0, e, :, cols], preferred_element_type=f32)
                u = jnp.dot(x, w_in[1, e, :, cols], preferred_element_type=f32)
                hid[e, :, cols] = (jax.nn.silu(g) * u).astype(bf16)
        gates = []
        for e in range(n_exp):
            parts = []
            for part in (0, 1):
                for side in (RIGHT, LEFT):
                    start = (part * 2 + jnp.where(fresh, side, 1 - side)) * quarter
                    col = side * n_exp + e
                    parts.append(gate_col[kind, pl.ds(pl.multiple_of(start, quarter), quarter), col : col + 1])
            gates.append(jnp.concatenate(parts, axis=0))
        for b in range(d_model // blk):
            cols = pl.ds(b * blk, blk)
            z = None
            for e in range(n_exp):
                y = jnp.dot(hid[e], wd[e, :, cols], preferred_element_type=f32)
                y = y.astype(bf16).astype(f32)
                term = jnp.where(gates[e] != 0.0, gates[e] * y, 0.0)
                z = term if z is None else z + term
            zbuf[i, krows(kind), cols] = z.astype(bf16)

    def prepare(ahead):
        pairs = [(kind, way) for kind in (0, 1) for way in ((RIGHT,) if ahead == far else (RIGHT, LEFT))]
        masks = [routed(experts_ahead(ahead, way, kind), me) for kind, way in pairs]
        rank = ranks(masks)
        for j, (kind, way) in enumerate(pairs):
            picks[kind, (ahead - far + 2) * 2 + way] = packer(masks[j], rank[j : j + 1]).astype(bf16)

    def send_leaves(pairs):
        packed = []
        for n, kind in pairs:
            length, _ = sends[n]
            for way in (RIGHT, LEFT):
                ahead, toward = (length, way) if length <= far else (n_chips - length, 1 - way)
                pick = picks[kind, (ahead - far + 2) * 2 + (RIGHT if ahead == far else toward)]
                cols = pl.ds(group_of(length, way) * wide, wide)
                z = jnp.concatenate([zbuf[i, rows(kind, part, side), cols] for i, part, side in place(length, way)], axis=0)
                packed.append((n, way, kind, jnp.dot(pick, z, preferred_element_type=f32)))
        for n, way, kind, z in packed:
            packbuf[n, way, kind] = z.astype(bf16)
        for n, way, kind, _ in packed:
            leaf_copy(n, way, kind).start()

    def fresh_hop(i, move):
        @pl.when((lax.rem(i, 2) == 1) | (i == 0))
        def _():
            move((i + 1) // 2)

    def step(turn, carry):
        i = turn // 2
        even = lax.rem(turn, 2) == 0

        @pl.when(even)
        def _():
            @pl.when(i >= 1)
            def _():
                arrive(i, 1)

            xd_copy(i, core).start()
            fresh_hop(i, lambda hop: md_copy(hop, core).start())

        @pl.when(jnp.logical_not(even))
        def _():
            @pl.when(i < last)
            def _():
                arrive(i + 1, 0)

            fresh_hop(i, lambda hop: md_copy(hop, 1 - core).wait_recv())

            @pl.when(i == last)
            def _():
                prepare(far)

            xd_copy(i, 1 - core).wait_recv()

        kind = jnp.where(even, core, 1 - core)
        compute(i, kind)

        @pl.when(jnp.logical_not(even))
        def _():
            zd_copy(i).start()

        @pl.when(turn == 2 * last - 7)
        def _():
            prepare(far - 2)

        @pl.when(turn == 2 * last - 4)
        def _():
            send_leaves([(0, 0), (0, 1)])

        @pl.when(turn == 2 * last - 3)
        def _():
            prepare(far - 1)

        @pl.when((turn == 2 * last - 2) | (turn == 2 * last - 1))
        def _():
            send_leaves([(1, kind), (2, kind)])

        @pl.when(turn == 2 * last + 1)
        def _():
            send_leaves([(3, 0), (3, 1)])

        return carry

    lax.fori_loop(0, 2 * last + 2, step, 0)

    def unpack(n, way):
        ahead = sends[n][0] - 1
        expert = experts_ahead(ahead, way, core)
        masks = [routed(expert, next_chip[1 - way] * 2 + k) for k in (0, 1)]
        rank = ranks(masks)
        spread = [packer(masks[k], rank[k : k + 1]).T.astype(bf16) for k in (0, 1)]
        if way == RIGHT:
            drain(leafbuf.at[n], lf_recv.at[n])
        return sum(jnp.dot(spread[k], leafbuf[n, way, k], preferred_element_type=f32) for k in (0, 1))

    def own_part(ahead, way, cols):
        parts = [
            zbuf[i, rows(core, part, side), cols].astype(f32) + zpart[i, rows(0, part, side), cols].astype(f32)
            for i, part, side in place(ahead, way)
        ]
        return jnp.concatenate(parts, axis=0)

    drain(zpart.at[:last], zd_recv.at[0])
    for n in range(n_leaf, len(sends)):
        length, ahead = sends[n]
        src = sends.index((length, ahead + 1))
        if ahead == far:
            drain(zpart.at[last], zd_recv.at[1])
        for way in (RIGHT, LEFT):
            own = own_part(ahead, way, pl.ds(group_of(length, way) * wide, wide))
            if src < n_leaf:
                came = unpack(src, way)
            else:
                if way == RIGHT:
                    drain(recvbuf.at[src - n_leaf], rs_recv.at[src - n_leaf])
                came = recvbuf[src - n_leaf, way]
            sumbuf[n - n_leaf, way] = came + own
            rs_copy(n, way).start()

    ends = [n for n in range(len(sends)) if sends[n][1] == 1]
    known = set()
    for n in ends[2:]:
        for way in (RIGHT, LEFT):
            length = sends[n][0]
            group = group_of(length, way)
            other = sends.index((n_chips - 1 - length, 1))
            cols = pl.ds(group * wide, wide)
            own = own_part(0, way, cols)
            for m in (other, n):
                if m not in known:
                    known.add(m)
                    drain(recvbuf.at[m - n_leaf], rs_recv.at[m - n_leaf])
            came = recvbuf[n - n_leaf, way] + recvbuf[other - n_leaf, 1 - way]
            out_ref[:, cols] = (came + own).astype(out_ref.dtype)

    drain(xbuf.at[1:, :n_tok], ag_send)
    drain(meta.at[:far, 0], mt_send)
    drain(xbuf.at[:, :n_tok], xd_send)
    drain(meta.at[:, 0], md_send)
    drain(zpart, zd_send)
    drain(packbuf, lf_send)
    drain(sumbuf, rs_send)


def solution(mesh):
    groups = mesh.shape[AXIS]
    n_chips = groups // 2
    far = n_chips // 2
    last = 2 * far - 1
    n_sums = len(chain_order(far)) - 4
    row_spec = P(("data", "expert"), None)
    weight_spec = P("expert", None, None)

    def device_layer(tokens, expert_ids, gate_wts, dev_slot, exp_slot, w_gate, w_up, w_down):
        tok_dev, top_k = expert_ids.shape
        d_model = tokens.shape[1]
        e_local, _, d_ff = w_gate.shape
        dev_cap = min(tok_dev, 8 * ((3 * tok_dev * top_k + 16 * groups - 1) // (16 * groups)))
        bf16, f32, i32 = jnp.bfloat16, jnp.float32, jnp.int32
        dma = pltpu.SemaphoreType.DMA
        args = (tokens, expert_ids.T, gate_wts.T, dev_slot.T, exp_slot.T, w_gate, w_up, w_down)
        args = [pltpu.with_memory_space_constraint(a, pltpu.HBM) for a in args]
        return pl.pallas_call(
            functools.partial(moe_kernel, n_chips),
            out_shape=jax.ShapeDtypeStruct((tok_dev, d_model), bf16),
            in_specs=[pl.BlockSpec(memory_space=pltpu.HBM)] * len(args),
            out_specs=pl.BlockSpec(memory_space=pltpu.VMEM),
            scratch_shapes=[
                pltpu.VMEM((last + 1, 2 * tok_dev, d_model), bf16),
                pltpu.VMEM((last + 1, 2 * tok_dev, d_model), bf16),
                pltpu.VMEM((last + 1, tok_dev, d_model), bf16),
                pltpu.VMEM((4, 2, 2, dev_cap, d_model // 4), bf16),
                pltpu.VMEM((4, 2, 2, dev_cap, d_model // 4), bf16),
                pltpu.VMEM((n_sums, 2, tok_dev, d_model // 4), f32),
                pltpu.VMEM((n_sums, 2, tok_dev, d_model // 4), f32),
                pltpu.VMEM((far + 1, 2, 2, 2 * top_k, tok_dev), bf16),
                pltpu.VMEM((2, tok_dev, 128), f32),
                pltpu.VMEM((2, 5, dev_cap, tok_dev), bf16),
                pltpu.VMEM((e_local, tok_dev, d_ff), bf16),
                pltpu.VMEM((2, *w_gate.shape), bf16),
                pltpu.VMEM(w_down.shape, bf16),
                pltpu.VMEM((top_k, tok_dev), i32),
                pltpu.VMEM((top_k, tok_dev), f32),
                pltpu.VMEM((top_k, tok_dev), i32),
                pltpu.VMEM((top_k, tok_dev), i32),
                dma((4,)),
                dma, dma((last, 2)),
                dma, dma((far,)),
                dma, dma((last + 1,)),
                dma, dma((far + 1,)),
                dma, dma((2,)),
                dma, dma((4,)),
                dma, dma((n_sums,)),
            ],
            compiler_params=pltpu.CompilerParams(
                collective_id=0, has_side_effects=True, vmem_limit_bytes=48 * 1024 * 1024
            ),
        )(*args)

    def moe_layer(tokens, expert_ids, gate_wts, dev_slot, exp_slot, w_gate, w_up, w_down):
        mapped = jax.shard_map(device_layer, mesh=mesh, in_specs=(row_spec,) * 5 + (weight_spec,) * 3, out_specs=row_spec, check_vma=False)
        return mapped(tokens, expert_ids, gate_wts, dev_slot, exp_slot, w_gate, w_up, w_down)

    return moe_layer
```

time: 69.8 us -> 68.5 us (0.981)
  Pallas kernels: 69 us -> 67.8 us
    pallas_call x1, Pallas kernels: 69 us -> 67.8 us  [device_layer(): pl.pallas_call(functools.partial(moe_kernel, n_chips), out_shape=jax.Shap...]
where the time goes in v4:
time: 68.5 us
  Pallas kernels  67.8 us (99%)
  local copies, waits for them, and re-layouts  0.71 us (1%)
    pallas_call x1, Pallas kernels, device_layer(): pl.pallas_call(functools.partial(moe_kernel, n_chips), out_shape=jax.Shap...  67.8 us

profile of v4, /device:TPU:21, one launch (start us, length us, event | category | flops | bytes accessed | tf_op | source)
XLA Modules:
  0.0 68.5 jit_solution(4543294235964836513)
XLA Ops:
  0.0 67.8 %shard_map.82 = bf16[128,1024]{1,0:T(8,128)(2,1)S(1)} custom-call(bf16[128,1024]{1,0:T(8,128)(2,1)} %tok_hbm.1, s32[8,128]{1,0:T(8,128)} %bitcast.4, f32[8,128]{1,0:T(8,128)} %bitcast.5, s32[8,128]{1,0:T(8,128)} %bitcast.6, s32[8,128]{1,0:T(8,128)} %bitcast.7, bf16[2,1024,512]{2,1,0:T(8,128)(2,1)} %wg_hbm.1, bf16[2,1024,512]{2,1,0:T(8,128)(2,1)} %wu_hbm.1, ...), custom_call_target="tpu_custom_call" | custom-call | tf_op jit(solution)/shard_map/pallas_call | solution.py:388
  67.8 0.7 %copy.10 = bf16[128,1024]{1,0:T(8,128)(2,1)} copy(bf16[128,1024]{1,0:T(8,128)(2,1)S(1)} %shard_map.82) | data formatting | bytes 524288

commit v5 on v4

--- a/solution.py
+++ b/solution.py
@@ -13,10 +13,10 @@
 
 
 def chain_order(far):
-    a, b, c, d = far + 1, far - 1, far, far - 2
-    assert d == 2
+    a, b, c, d = far + 2, far - 1, far, far - 3
+    assert d == 1
     return [
-(d, 2), (b, 3), (a, 5), (c, 4), (b, 2), (a, 4), (c, 3), (b, 1), (a, 3), (c, 2), (a, 2), (d, 1), (c, 1), (a, 1),
+        (a, 6), (d, 1), (b, 3), (c, 4), (a, 5), (b, 2), (a, 4), (c, 3), (b, 1), (a, 3), (c, 2), (a, 2), (c, 1), (a, 1),
     ]
 
 
@@ -24,7 +24,7 @@
     n_chips,
     tok_hbm, ids_hbm, wts_hbm, dslot_hbm, eslot_hbm, wg_hbm, wu_hbm, wd_hbm,
     out_ref,
-    xbuf, zbuf, zpart, packbuf, leafbuf, sumbuf, recvbuf, meta, gate_col, picks, hid, w_in, wd, ids, wts, dslot, eslot,
+    xbuf, zbuf, zpart, packbuf, leafbuf, sumbuf, recvbuf, meta, gate_col, picks, direct, hid, w_in, wd, ids, wts, dslot, eslot,
     load_sem, ag_send, ag_recv, mt_send, mt_recv, xd_send, xd_recv, md_send, md_recv,
     zd_send, zd_recv, lf_send, lf_recv, rs_send, rs_recv,
 ):
@@ -80,7 +80,7 @@
         return remote(zbuf.at[i, krows(1 - core)], zpart.at[i], zd_send, zd_recv.at[i // last], mate)
 
     def group_of(length, way):
-        order = (far, far - 1, far + 1, far - 2)
+        order = (far, far - 1, far + 2, far - 3)
         return order.index(length if way == RIGHT else n_chips - 1 - length)
 
     def leaf_copy(n, way, kind):
@@ -228,7 +228,7 @@
         masks = [routed(experts_ahead(ahead, way, kind), me) for kind, way in pairs]
         rank = ranks(masks)
         for j, (kind, way) in enumerate(pairs):
-            picks[kind, (ahead - far + 2) * 2 + way] = packer(masks[j], rank[j : j + 1]).astype(bf16)
+            picks[kind, (ahead - 1) * 2 + way] = packer(masks[j], rank[j : j + 1]).astype(bf16)
 
     def send_leaves(pairs):
         packed = []
@@ -236,7 +236,7 @@
             length, _ = sends[n]
             for way in (RIGHT, LEFT):
                 ahead, toward = (length, way) if length <= far else (n_chips - length, 1 - way)
-                pick = picks[kind, (ahead - far + 2) * 2 + (RIGHT if ahead == far else toward)]
+                pick = picks[kind, (ahead - 1) * 2 + (RIGHT if ahead == far else toward)]
                 cols = pl.ds(group_of(length, way) * wide, wide)
                 z = jnp.concatenate([zbuf[i, rows(kind, part, side), cols] for i, part, side in place(length, way)], axis=0)
                 packed.append((n, way, kind, jnp.dot(pick, z, preferred_element_type=f32)))
@@ -244,69 +244,6 @@
             packbuf[n, way, kind] = z.astype(bf16)
         for n, way, kind, _ in packed:
             leaf_copy(n, way, kind).start()
-
-    def fresh_hop(i, move):
-        @pl.when((lax.rem(i, 2) == 1) | (i == 0))
-        def _():
-            move((i + 1) // 2)
-
-    def step(turn, carry):
-        i = turn // 2
-        even = lax.rem(turn, 2) == 0
-
-        @pl.when(even)
-        def _():
-            @pl.when(i >= 1)
-            def _():
-                arrive(i, 1)
-
-            xd_copy(i, core).start()
-            fresh_hop(i, lambda hop: md_copy(hop, core).start())
-
-        @pl.when(jnp.logical_not(even))
-        def _():
-            @pl.when(i < last)
-            def _():
-                arrive(i + 1, 0)
-
-            fresh_hop(i, lambda hop: md_copy(hop, 1 - core).wait_recv())
-
-            @pl.when(i == last)
-            def _():
-                prepare(far)
-
-            xd_copy(i, 1 - core).wait_recv()
-
-        kind = jnp.where(even, core, 1 - core)
-        compute(i, kind)
-
-        @pl.when(jnp.logical_not(even))
-        def _():
-            zd_copy(i).start()
-
-        @pl.when(turn == 2 * last - 7)
-        def _():
-            prepare(far - 2)
-
-        @pl.when(turn == 2 * last - 4)
-        def _():
-            send_leaves([(0, 0), (0, 1)])
-
-        @pl.when(turn == 2 * last - 3)
-        def _():
-            prepare(far - 1)
-
-        @pl.when((turn == 2 * last - 2) | (turn == 2 * last - 1))
-        def _():
-            send_leaves([(1, kind), (2, kind)])
-
-        @pl.when(turn == 2 * last + 1)
-        def _():
-            send_leaves([(3, 0), (3, 1)])
-
-        return carry
-
-    lax.fori_loop(0, 2 * last + 2, step, 0)
 
     def unpack(n, way):
         ahead = sends[n][0] - 1
@@ -325,8 +262,7 @@
         ]
         return jnp.concatenate(parts, axis=0)
 
-    drain(zpart.at[:last], zd_recv.at[0])
-    for n in range(n_leaf, len(sends)):
+    def back(n):
         length, ahead = sends[n]
         src = sends.index((length, ahead + 1))
         if ahead == far:
@@ -342,9 +278,81 @@
             sumbuf[n - n_leaf, way] = came + own
             rs_copy(n, way).start()
 
+    def fresh_hop(i, move):
+        @pl.when((lax.rem(i, 2) == 1) | (i == 0))
+        def _():
+            move((i + 1) // 2)
+
+    def step(turn, carry):
+        i = turn // 2
+        even = lax.rem(turn, 2) == 0
+
+        @pl.when(even)
+        def _():
+            @pl.when(i >= 1)
+            def _():
+                arrive(i, 1)
+
+            xd_copy(i, core).start()
+            fresh_hop(i, lambda hop: md_copy(hop, core).start())
+
+        @pl.when(jnp.logical_not(even))
+        def _():
+            @pl.when(i < last)
+            def _():
+                arrive(i + 1, 0)
+
+            fresh_hop(i, lambda hop: md_copy(hop, 1 - core).wait_recv())
+
+            @pl.when(i == last)
+            def _():
+                prepare(far)
+
+            xd_copy(i, 1 - core).wait_recv()
+
+        kind = jnp.where(even, core, 1 - core)
+        compute(i, kind)
+
+        @pl.when(jnp.logical_not(even))
+        def _():
+            zd_copy(i).start()
+
+        @pl.when(turn == 2 * last - 7)
+        def _():
+            prepare(far - 3)
+            prepare(far - 2)
+
+        @pl.when(turn == 2 * last - 4)
+        def _():
+            send_leaves([(0, 0), (0, 1)])
+            send_leaves([(1, 0), (1, 1)])
+
+        @pl.when(turn == 2 * last - 3)
+        def _():
+            prepare(far - 1)
+
+        @pl.when((turn == 2 * last - 2) | (turn == 2 * last - 1))
+        def _():
+            send_leaves([(2, kind)])
+
+        @pl.when(turn == 2 * last + 1)
+        def _():
+            send_leaves([(3, 0), (3, 1)])
+
+        return carry
+
+    lax.fori_loop(0, 2 * last + 2, step, 0)
+
+    drain(zpart.at[:last], zd_recv.at[0])
+    for n in range(n_leaf, len(sends)):
+        back(n)
+        if n == n_leaf + 2:
+            for way in (RIGHT, LEFT):
+                direct[way] = unpack(1, way)
+
     ends = [n for n in range(len(sends)) if sends[n][1] == 1]
     known = set()
-    for n in ends[2:]:
+    for n in ends[-2:]:
         for way in (RIGHT, LEFT):
             length = sends[n][0]
             group = group_of(length, way)
@@ -352,10 +360,10 @@
             cols = pl.ds(group * wide, wide)
             own = own_part(0, way, cols)
             for m in (other, n):
-                if m not in known:
+                if m >= n_leaf and m not in known:
                     known.add(m)
                     drain(recvbuf.at[m - n_leaf], rs_recv.at[m - n_leaf])
-            came = recvbuf[n - n_leaf, way] + recvbuf[other - n_leaf, 1 - way]
+            came = recvbuf[n - n_leaf, way] + (direct[1 - way] if other < n_leaf else recvbuf[other - n_leaf, 1 - way])
             out_ref[:, cols] = (came + own).astype(out_ref.dtype)
 
     drain(xbuf.at[1:, :n_tok], ag_send)
@@ -400,7 +408,8 @@
                 pltpu.VMEM((n_sums, 2, tok_dev, d_model // 4), f32),
                 pltpu.VMEM((far + 1, 2, 2, 2 * top_k, tok_dev), bf16),
                 pltpu.VMEM((2, tok_dev, 128), f32),
-                pltpu.VMEM((2, 5, dev_cap, tok_dev), bf16),
+                pltpu.VMEM((2, last, dev_cap, tok_dev), bf16),
+                pltpu.VMEM((2, tok_dev, d_model // 4), f32),
                 pltpu.VMEM((e_local, tok_dev, d_ff), bf16),
                 pltpu.VMEM((2, *w_gate.shape), bf16),
                 pltpu.VMEM(w_down.shape, bf16),

time: 68.5 us -> 67.9 us (level)
  Pallas kernels: 67.8 us -> 67 us
    pallas_call x1, Pallas kernels: 67.8 us -> 67 us  [device_layer(): pl.pallas_call(functools.partial(moe_kernel, n_chips), out_shape=jax.Shap...]
where the time goes in v5:
time: 67.9 us; the launch traced here: 67.7 us
  Pallas kernels  67 us (99%)
  local copies, waits for them, and re-layouts  0.71 us (1%)
    pallas_call x1, Pallas kernels, device_layer(): pl.pallas_call(functools.partial(moe_kernel, n_chips), out_shape=jax.Shap...  67 us

profile of v5, /device:TPU:21, one launch (start us, length us, event | category | flops | bytes accessed | tf_op | source)
XLA Modules:
  0.0 67.7 jit_solution(15272579852205964416)
XLA Ops:
  0.0 67.0 %shard_map.82 = bf16[128,1024]{1,0:T(8,128)(2,1)S(1)} custom-call(bf16[128,1024]{1,0:T(8,128)(2,1)} %tok_hbm.1, s32[8,128]{1,0:T(8,128)} %bitcast.4, f32[8,128]{1,0:T(8,128)} %bitcast.5, s32[8,128]{1,0:T(8,128)} %bitcast.6, s32[8,128]{1,0:T(8,128)} %bitcast.7, bf16[2,1024,512]{2,1,0:T(8,128)(2,1)} %wg_hbm.1, bf16[2,1024,512]{2,1,0:T(8,128)(2,1)} %wu_hbm.1, ...), custom_call_target="tpu_custom_call" | custom-call | tf_op jit(solution)/shard_map/pallas_call | solution.py:396
  67.0 0.7 %copy.10 = bf16[128,1024]{1,0:T(8,128)(2,1)} copy(bf16[128,1024]{1,0:T(8,128)(2,1)S(1)} %shard_map.82) | data formatting | bytes 524288

commit v6 on v5

--- a/solution.py
+++ b/solution.py
@@ -307,6 +307,7 @@
             @pl.when(i == last)
             def _():
                 prepare(far)
+                send_leaves([(3, core)])
 
             xd_copy(i, 1 - core).wait_recv()
 
@@ -337,7 +338,7 @@
 
         @pl.when(turn == 2 * last + 1)
         def _():
-            send_leaves([(3, 0), (3, 1)])
+            send_leaves([(3, 1 - core)])
 
         return carry
 

time: 67.9 us -> 67.8 us (level); the launches traced: 67.7 us -> 66.5 us
  Pallas kernels: 67 us -> 65.8 us
    pallas_call x1, Pallas kernels: 67 us -> 65.8 us  [device_layer(): pl.pallas_call(functools.partial(moe_kernel, n_chips), out_shape=jax.Shap...]
where the time goes in v6:
time: 67.8 us; the launch traced here: 66.5 us
  Pallas kernels  65.8 us (97%)
  local copies, waits for them, and re-layouts  0.71 us (1%)
    pallas_call x1, Pallas kernels, device_layer(): pl.pallas_call(functools.partial(moe_kernel, n_chips), out_shape=jax.Shap...  65.8 us

profile of v6, /device:TPU:21, one launch (start us, length us, event | category | flops | bytes accessed | tf_op | source)
XLA Modules:
  0.0 66.5 jit_solution(6746082482147836104)
XLA Ops:
  0.0 65.8 %shard_map.82 = bf16[128,1024]{1,0:T(8,128)(2,1)S(1)} custom-call(bf16[128,1024]{1,0:T(8,128)(2,1)} %tok_hbm.1, s32[8,128]{1,0:T(8,128)} %bitcast.4, f32[8,128]{1,0:T(8,128)} %bitcast.5, s32[8,128]{1,0:T(8,128)} %bitcast.6, s32[8,128]{1,0:T(8,128)} %bitcast.7, bf16[2,1024,512]{2,1,0:T(8,128)(2,1)} %wg_hbm.1, bf16[2,1024,512]{2,1,0:T(8,128)(2,1)} %wu_hbm.1, ...), custom_call_target="tpu_custom_call" | custom-call | tf_op jit(solution)/shard_map/pallas_call | solution.py:397
  65.8 0.7 %copy.10 = bf16[128,1024]{1,0:T(8,128)(2,1)} copy(bf16[128,1024]{1,0:T(8,128)(2,1)S(1)} %shard_map.82) | data formatting | bytes 524288

commit v7 on v6

--- a/solution.py
+++ b/solution.py
@@ -61,7 +61,7 @@
     def ag_copy(step, way, part, src_i, src_side):
         return remote(
             xbuf.at[src_i, rows(core, part, src_side)], xbuf.at[step + 1, rows(core, part, way)],
-            ag_send, ag_recv.at[step, part], next_chip[way] * 2 + core,
+            ag_send, ag_recv.at[step % 4, part], next_chip[way] * 2 + core,
         )
 
     def mt_copy(hop, way):
@@ -71,7 +71,7 @@
         )
 
     def xd_copy(i, kind):
-        return remote(xbuf.at[i, krows(kind)], xbuf.at[i, krows(kind)], xd_send, xd_recv.at[i], mate)
+        return remote(xbuf.at[i, krows(kind)], xbuf.at[i, krows(kind)], xd_send, xd_recv.at[lax.rem(i, 2)], mate)
 
     def md_copy(hop, kind):
         return remote(meta.at[hop, kind], meta.at[hop, kind], md_send, md_recv.at[hop], mate)
@@ -162,7 +162,7 @@
         return experts_of(ahead, kind, 1 - way) if ahead < far else experts_of(n_chips - ahead, kind, way)
 
     def arrive(i, part):
-        drain(xbuf.at[i, both_sides(core, part)], ag_recv.at[i - 1, part])
+        drain(xbuf.at[i, both_sides(core, part)], ag_recv.at[lax.rem(i - 1, 4), part])
 
         @pl.when(i <= last - 2)
         def _():
@@ -419,9 +419,9 @@
                 pltpu.VMEM((top_k, tok_dev), i32),
                 pltpu.VMEM((top_k, tok_dev), i32),
                 dma((4,)),
-                dma, dma((last, 2)),
+                dma, dma((4, 2)),
                 dma, dma((far,)),
-                dma, dma((last + 1,)),
+                dma, dma((2,)),
                 dma, dma((far + 1,)),
                 dma, dma((2,)),
                 dma, dma((4,)),

time: 67.8 us -> 67.7 us (level)
  no operation moved by 1% of the time
where the time goes in v7:
time: 67.7 us; the launch traced here: 66.4 us
  Pallas kernels  65.7 us (97%)
  local copies, waits for them, and re-layouts  0.71 us (1%)
    pallas_call x1, Pallas kernels, device_layer(): pl.pallas_call(functools.partial(moe_kernel, n_chips), out_shape=jax.Shap...  65.7 us

profile of v7, /device:TPU:21, one launch (start us, length us, event | category | flops | bytes accessed | tf_op | source)
XLA Modules:
  0.0 66.4 jit_solution(5810882226418568785)
XLA Ops:
  0.0 65.7 %shard_map.82 = bf16[128,1024]{1,0:T(8,128)(2,1)S(1)} custom-call(bf16[128,1024]{1,0:T(8,128)(2,1)} %tok_hbm.1, s32[8,128]{1,0:T(8,128)} %bitcast.4, f32[8,128]{1,0:T(8,128)} %bitcast.5, s32[8,128]{1,0:T(8,128)} %bitcast.6, s32[8,128]{1,0:T(8,128)} %bitcast.7, bf16[2,1024,512]{2,1,0:T(8,128)(2,1)} %wg_hbm.1, bf16[2,1024,512]{2,1,0:T(8,128)(2,1)} %wu_hbm.1, ...), custom_call_target="tpu_custom_call" | custom-call | tf_op jit(solution)/shard_map/pallas_call | solution.py:397
  65.7 0.7 %copy.10 = bf16[128,1024]{1,0:T(8,128)(2,1)} copy(bf16[128,1024]{1,0:T(8,128)(2,1)S(1)} %shard_map.82) | data formatting | bytes 524288
